TPU v7x, 128 devices: a whole 4x4x4 slice. The times are simulated.
128 devices in a mesh: replica: 1, dp: 128 (over z, y, x, core).
Axes of the slice: x: 4, y: 4, z: 4, core: 2. Of those that a mesh axis runs over, the one named last changes fastest.
Arguments:
- x_rows: bfloat16 [256, 2048], P(('replica', 'dp'))
- lengths: int32 [256], P(('replica', 'dp'))
- cache0: bfloat16 [256, 1024, 576], P(('replica', 'dp'))
- cache1: bfloat16 [256, 1024, 576], P(('replica', 'dp'))
- attn_gain: float32 [2, 2048], replicated
- w_dkv: bfloat16 [2, 2048, 576], replicated
- kv_gain: float32 [2, 512], replicated
- wq_a: bfloat16 [2, 2048, 768], replicated
- q_gain: float32 [2, 768], replicated
- wq_b: bfloat16 [2, 768, 5120], replicated
- w_uk: bfloat16 [2, 20, 192, 512], replicated
- w_uv: bfloat16 [2, 20, 512, 256], replicated
- w_o: bfloat16 [2, 5120, 2048], replicated
- ffn_gain: float32 [2, 2048], replicated
- w_gate: bfloat16 [2, 2048, 10240], replicated
- w_up: bfloat16 [2, 2048, 10240], replicated
- w_down: bfloat16 [2, 10240, 2048], replicated
Outputs:
- output 1: bfloat16 [256, 2048], P('replica')
- output 2: bfloat16 [256, 1024, 576], P(('replica', 'dp'))
- output 3: bfloat16 [256, 1024, 576], P(('replica', 'dp'))
All inputs are finite; a program needn't handle non-finite values.
Results may differ from a plain program's by a relative error of at most 0.02.
Values are sent between devices in bfloat16 or wider.
A program may use at most 1.5 GiB of HBM per device.

v0:
```python
import jax
import jax.numpy as jnp
from jax import lax
from jax.sharding import PartitionSpec as P


def rms_norm(values, gain_vec):
    return values * lax.rsqrt(jnp.mean(values * values, axis=-1, keepdims=True) + 1e-6) * gain_vec


def apply_rope(values, positions):
    half_dim = values.shape[-1] // 2
    inv_freq = 10000.0 ** (-jnp.arange(half_dim, dtype=jnp.float32) / half_dim)
    angles = positions.astype(jnp.float32)[..., None] * inv_freq
    cos_a = jnp.cos(angles)
    sin_a = jnp.sin(angles)
    first_half = values[..., :half_dim]
    second_half = values[..., half_dim:]
    return jnp.concatenate([first_half * cos_a - second_half * sin_a, second_half * cos_a + first_half * sin_a], axis=-1)


def mla_attention(residual, lengths, layer_cache, attn_gain, w_dkv, kv_gain, wq_a, q_gain, wq_b, w_uk, w_uv, w_o):
    num_rows = residual.shape[0]
    seq_len = layer_cache.shape[1]
    num_heads, nope_dim, kv_rank = w_uk.shape
    qk_dim = wq_b.shape[1] // num_heads
    hidden = rms_norm(residual.astype(jnp.float32), attn_gain).astype(jnp.bfloat16)
    kv_proj = jnp.dot(hidden, w_dkv, preferred_element_type=jnp.float32)
    latent = rms_norm(kv_proj[:, :kv_rank], kv_gain).astype(jnp.bfloat16)
    key_rope = apply_rope(kv_proj[:, kv_rank:], lengths).astype(jnp.bfloat16)
    new_entry = jnp.concatenate([latent, key_rope], axis=-1)
    slot_ids = lax.broadcasted_iota(jnp.int32, (1, seq_len), 1)
    at_slot = slot_ids == lengths[:, None]
    cache_new = jnp.where(at_slot[:, :, None], new_entry[:, None, :], layer_cache)
    q_low = rms_norm(jnp.dot(hidden, wq_a, preferred_element_type=jnp.float32), q_gain).astype(jnp.bfloat16)
    queries = jnp.dot(q_low, wq_b, preferred_element_type=jnp.float32).astype(jnp.bfloat16).reshape(num_rows, num_heads, qk_dim)
    q_rope = apply_rope(queries[:, :, nope_dim:].astype(jnp.float32), lengths[:, None]).astype(jnp.bfloat16)
    q_latent = jnp.einsum('bhn,hnk->bhk', queries[:, :, :nope_dim], w_uk, preferred_element_type=jnp.float32).astype(jnp.bfloat16)
    q_full = jnp.concatenate([q_latent, q_rope], axis=-1)
    scores = jnp.einsum('bhc,btc->bht', q_full, cache_new, preferred_element_type=jnp.float32) * (qk_dim ** -0.5)
    visible = slot_ids <= lengths[:, None]
    scores = jnp.where(visible[:, None, :], scores, -1e30)
    attn_probs = jax.nn.softmax(scores, axis=-1).astype(jnp.bfloat16)
    out_latent = jnp.einsum('bht,btk->bhk', attn_probs, cache_new[:, :, :kv_rank], preferred_element_type=jnp.float32).astype(jnp.bfloat16)
    heads_out = jnp.einsum('cil,ilw->ciw', out_latent, w_uv, preferred_element_type=jnp.float32).astype(jnp.bfloat16).reshape(num_rows, -1)
    attn_out = jnp.dot(heads_out, w_o, preferred_element_type=jnp.float32)
    return (residual.astype(jnp.float32) + attn_out).astype(jnp.bfloat16), cache_new


def mlp_partial(normed, w_gate, w_up, w_down):
    gate_proj = jnp.dot(normed, w_gate, preferred_element_type=jnp.float32)
    up_proj = jnp.dot(normed, w_up, preferred_element_type=jnp.float32)
    activated = (jax.nn.silu(gate_proj) * up_proj).astype(jnp.bfloat16)
    return jnp.dot(activated, w_down, preferred_element_type=jnp.float32)


def solution(mesh):
    group_size = mesh.shape['dp']
    row_spec = P(('replica', 'dp'), None)
    len_spec = P(('replica', 'dp'))
    cache_spec = P(('replica', 'dp'), None, None)
    repl_spec = P()
    col_spec = P(None, None, 'dp')
    down_spec = P(None, 'dp', None)
    in_specs = (row_spec, len_spec, cache_spec, cache_spec, repl_spec, repl_spec, repl_spec, repl_spec, repl_spec, repl_spec, repl_spec, repl_spec, repl_spec, repl_spec, col_spec, col_spec, down_spec)
    out_specs = (P('replica', None), cache_spec, cache_spec)

    def device_step(x_rows, lengths, cache0, cache1, attn_gain, w_dkv, kv_gain, wq_a, q_gain, wq_b, w_uk, w_uv, w_o, ffn_gain, w_gate, w_up, w_down):
        residual = x_rows
        num_rows, model_dim = residual.shape
        new_caches = []
        for layer_idx, layer_cache in enumerate((cache0, cache1)):
            residual, cache_new = mla_attention(residual, lengths, layer_cache, attn_gain[layer_idx], w_dkv[layer_idx], kv_gain[layer_idx], wq_a[layer_idx], q_gain[layer_idx], wq_b[layer_idx], w_uk[layer_idx], w_uv[layer_idx], w_o[layer_idx])
            new_caches.append(cache_new)
            normed = rms_norm(residual.astype(jnp.float32), ffn_gain[layer_idx]).astype(jnp.bfloat16)
            all_normed = lax.all_gather(normed, 'dp', axis=0, tiled=True)
            part_sums = mlp_partial(all_normed, w_gate[layer_idx], w_up[layer_idx], w_down[layer_idx]).astype(jnp.bfloat16)
            received = lax.all_to_all(part_sums, 'dp', 0, 0, tiled=True)
            mlp_out = jnp.sum(received.reshape(group_size, num_rows, model_dim).astype(jnp.float32), axis=0)
            residual = (residual.astype(jnp.float32) + mlp_out).astype(jnp.bfloat16)
        full_rows = lax.all_gather(residual, 'dp', axis=0, tiled=True)
        return full_rows, new_caches[0], new_caches[1]

    return jax.shard_map(device_step, mesh=mesh, in_specs=in_specs, out_specs=out_specs, check_vma=False)
```

profile of v0, /device:TPU:1, one launch (start us, length us, event | category | flops | bytes accessed | tf_op | source)
XLA Modules:
  0.0 343.5 jit_solution(14164005619883254966)
XLA Ops:
  11.8 2.4 fusion.40
  14.2 2.7 multiply_reduce_fusion.3
  17.2 4.7 %fusion.14 = bf16[2,5120]{1,0:T(2,128)(2,1)S(1)} fusion(bf16[2,768,5120]{2,1,0:T(8,128)(2,1)} %param.26, f32[2,768]{1,0:T(2,128)S(1)} %get-tuple-element.29, f32[2]{0:T(128)S(1)} %add_rsqrt_fusion.6, f32[768]{0:T(1024)S(1)} %get-tuple-element.7), kind=kOutput, calls=%fused_computation.14 | convolution fusion | flops 15743488 | bytes 7894024 | tf_op jit(solution)/shard_map/dot_general | solution.py:36
  22.6 2.6 copy.22
  29.1 3.3 fusion.92
  32.4 8.6 %multiply_reduce_fusion.1 = (f32[2]{0:T(128)S(1)}, f32[2,2048]{1,0:T(2,128)S(1)}) fusion(bf16[2,5120]{1,0:T(2,128)(2,1)S(1)} %bitcast.135, bf16[2,5120,2048]{2,1,0:T(8,128)(2,1)} %param.29, bf16[2,2048]{1,0:T(2,128)(2,1)S(1)} %copy-done.4), kind=kOutput, calls=%fused_computation.127 | convolution fusion | flops 41967616 | bytes 21016584 | tf_op jit(solution)/shard_map/dot_general | solution.py:46
  41.7 67.4 %all-gather.7.cloned.1.call-done = bf16[128,2,2048]{2,1,0:T(2,128)(2,1)} async-done(((bf16[1,2,2048]{2,1,0:T(2,128)(2,1)}), bf16[128,2,2048]{2,1,0:T(2,128)(2,1)}) %all-gather.7.cloned.1.call-update) | async-done | bytes 1048592 | tf_op jit(solution)/shard_map/all_gather | solution.py:76
  113.4 4.1 %convolution_convert_fusion.1 = bf16[256,2048]{1,0:T(8,128)(2,1)} fusion(bf16[256,2048]{1,0:T(8,128)(2,1)} %reshape.211, bf16[2,2048,10240]{2,1,0:T(8,128)(2,1)} %param.32, s32[]{:T(128)S(6)} %multiply.58, bf16[2,10240,2048]{2,1,0:T(8,128)(2,1)} %param.33, f32[256,80]{0,1:T(8,128)S(1)} %fusion.99), kind=kOutput, calls=%fused_computation.37 | convolution fusion | flops 168419328 | bytes 3032064 | tf_op jit(solution)/shard_map/dot_general | solution.py:54
  117.5 2.5 all_to_all.12
  120.0 5.8 %all-to-all-start = ((bf16[128,2,2048]{2,1,0:T(2,128)(2,1)}), bf16[128,2,2048]{2,1,0:T(2,128)(2,1)}, u32[]{:S(2)}, u32[]{:S(2)}) async-start(bf16[128,2,2048]{2,1,0:T(2,128)(2,1)} %all_to_all.12), calls=%async_computation | async-start | bytes 2097152 | tf_op jit(solution)/shard_map/all_to_all | solution.py:78
  126.1 4.3 %copy.28 = bf16[2,1024,576]{2,1,0:T(8,128)(2,1)} copy(bf16[2,1024,576]{1,2,0:T(8,128)(2,1)} %param.20) | data formatting | bytes 4718592 | tf_op args[3]
  130.4 14.1 %all-to-all-done = bf16[128,2,2048]{2,1,0:T(2,128)(2,1)} async-done(((bf16[128,2,2048]{2,1,0:T(2,128)(2,1)}), bf16[128,2,2048]{2,1,0:T(2,128)(2,1)}, u32[]{:S(2)}, u32[]{:S(2)}) %all-to-all-start) | async-done | bytes 1048608 | tf_op jit(solution)/shard_map/all_to_all | solution.py:78
  149.2 2.6 multiply_reduce_fusion.2
  152.0 4.5 %fusion.17 = bf16[2,5120]{1,0:T(2,128)(2,1)S(1)} fusion(bf16[2,768,5120]{2,1,0:T(8,128)(2,1)} %param.26, f32[2,768]{1,0:T(2,128)S(1)} %get-tuple-element.33, f32[2]{0:T(128)S(1)} %add_rsqrt_fusion.2, f32[768]{0:T(1024)S(1)} %get-tuple-element.6), kind=kOutput, calls=%fused_computation.15 | convolution fusion | flops 15743488 | bytes 7894024 | tf_op jit(solution)/shard_map/dot_general | solution.py:36
  156.6 2.7 fusion.86
  164.7 3.3 fusion.95
  168.0 8.6 %multiply_reduce_fusion = (f32[2]{0:T(128)S(1)}, f32[2,2048]{1,0:T(2,128)S(1)}) fusion(bf16[2,5120]{1,0:T(2,128)(2,1)S(1)} %bitcast.134, bf16[2,5120,2048]{2,1,0:T(8,128)(2,1)} %param.29, bf16[2,2048]{1,0:T(2,128)(2,1)S(1)} %get-tuple-element.9), kind=kOutput, calls=%fused_computation.124 | convolution fusion | flops 41967616 | bytes 21016584 | tf_op jit(solution)/shard_map/dot_general | solution.py:46
  177.3 60.1 %all-gather.9.cloned.1.call-done = bf16[128,2,2048]{2,1,0:T(2,128)(2,1)} async-done(((bf16[1,2,2048]{2,1,0:T(2,128)(2,1)}), bf16[128,2,2048]{2,1,0:T(2,128)(2,1)}) %all-gather.9.cloned.1.call-update) | async-done | bytes 1048592 | tf_op jit(solution)/shard_map/all_gather | solution.py:76
  241.9 4.1 %convolution_convert_fusion = bf16[256,2048]{1,0:T(8,128)(2,1)} fusion(bf16[256,2048]{1,0:T(8,128)(2,1)} %reshape.213, bf16[2,2048,10240]{2,1,0:T(8,128)(2,1)} %param.32, s32[]{:T(128)S(6)} %add.115, s32[]{:T(128)S(6)} %multiply.58, bf16[2,10240,2048]{2,1,0:T(8,128)(2,1)} %param.33, f32[256,80]{0,1:T(8,128)S(1)} %fusion.98), kind=kOutput, calls=%fused_computation.36 | convolution fusion | flops 168419328 | bytes 3033088 | tf_op jit(solution)/shard_map/dot_general | solution.py:54
  246.0 2.5 all_to_all.14
  248.5 24.4 %all_to_all.18 = bf16[128,2,2048]{2,1,0:T(2,128)(2,1)S(1)} all-to-all(bf16[128,2,2048]{2,1,0:T(2,128)(2,1)} %all_to_all.14), channel_id=1, replica_groups=mesh['replica'=1,'dp'=128] {'dp'}, dimensions={0} | all-to-all | bytes 2097152 | tf_op jit(solution)/shard_map/all_to_all | solution.py:78
  274.4 2.5 copy.32
  276.9 4.3 %copy.33 = bf16[2,1024,576]{1,2,0:T(8,128)(2,1)} copy(bf16[2,1024,576]{2,1,0:T(8,128)(2,1)} %copy-done) | data formatting | bytes 4718592
  281.2 53.5 %all-gather.11.cloned.1.call-done = bf16[128,2,2048]{2,1,0:T(2,128)(2,1)} async-done(((bf16[1,2,2048]{2,1,0:T(2,128)(2,1)}), bf16[128,2,2048]{2,1,0:T(2,128)(2,1)}) %all-gather.11.cloned.1.call-update) | async-done | bytes 1048592 | tf_op jit(solution)/shard_map/all_gather | solution.py:81
  (69 shorter events, 34.0 us)
Async XLA Ops:
  7.2 10.0 %copy-start.5 = (f32[2,2048]{1,0:T(2,128)S(1)}, f32[2,2048]{1,0:T(2,128)}, u32[]{:S(2)}) copy-start(f32[2,2048]{1,0:T(2,128)} %param.30) | copy-start | bytes 49156
  7.2 101.8 %all-gather.7.cloned.1.call-start = ((), (), s32[]{:S(2)}) async-start(), calls=%async_computation.2 | async-start | bytes 1056768 | tf_op jit(solution)/shard_map/all_gather | solution.py:76
  14.2 7.7 %copy-start.2 = (bf16[2,20,192,512]{3,2,1,0:T(8,128)(2,1)S(1)}, bf16[2,20,192,512]{3,2,1,0:T(8,128)(2,1)}, u32[]{:S(2)}) copy-start(bf16[2,20,192,512]{3,2,1,0:T(8,128)(2,1)} %param.27) | copy-start | bytes 23592964
  17.2 5.4 %copy-start.3 = (bf16[2,1024,576]{1,2,0:T(8,128)(2,1)S(1)}, bf16[2,1024,576]{1,2,0:T(8,128)(2,1)}, u32[]{:S(2)}) copy-start(bf16[2,1024,576]{1,2,0:T(8,128)(2,1)} %param.19) | copy-start | bytes 7077892
  27.6 4.7 %copy-start.4 = (bf16[2,2048]{1,0:T(2,128)(2,1)S(1)}, bf16[2,2048]{1,0:T(2,128)(2,1)}, u32[]{:S(2)}) copy-start(bf16[2,2048]{1,0:T(2,128)(2,1)} %param.17) | copy-start | bytes 24580
  120.0 24.5 %all-to-all-start = ((bf16[128,2,2048]{2,1,0:T(2,128)(2,1)}), bf16[128,2,2048]{2,1,0:T(2,128)(2,1)}, u32[]{:S(2)}, u32[]{:S(2)}) async-start(bf16[128,2,2048]{2,1,0:T(2,128)(2,1)} %all_to_all.12), calls=%async_computation | async-start | bytes 2097152 | tf_op jit(solution)/shard_map/all_to_all | solution.py:78
  125.9 111.6 %all-gather.9.cloned.1.call-start = ((), (), s32[]{:S(2)}) async-start(), calls=%async_computation.3 | async-start | bytes 1056768 | tf_op jit(solution)/shard_map/all_gather | solution.py:76
  152.0 7.6 %copy-start.1 = (bf16[2,1024,576]{2,1,0:T(8,128)(2,1)S(1)}, bf16[2,1024,576]{2,1,0:T(8,128)(2,1)}, u32[]{:S(2)}) copy-start(bf16[2,1024,576]{2,1,0:T(8,128)(2,1)} %copy.28) | copy-start | bytes 7077892
  160.2 1.5 copy-start
  177.3 157.4 %all-gather.11.cloned.1.call-start = ((), (), s32[]{:S(2)}) async-start(), calls=%async_computation.4 | async-start | bytes 1056768 | tf_op jit(solution)/shard_map/all_gather | solution.py:81
Sparse Core Ops, SparseCore 0:
  41.8 67.1 all-gather.6
  177.4 60.0 all-gather.8
  274.5 60.1 all-gather.10
where the time goes:
time: 345 us; the launch traced here: 343 us
  waiting for transfers between devices  195 us (57%)
  matrix products  62.9 us (18%)
  local copies, waits for them, and re-layouts  29.3 us (8%)
  blocking collectives  24.4 us (7%)
  between operations  13.9 us (4%)
  other arithmetic  11.6 us (3%)
  starting transfers between devices  6.14 us (2%)
    all_gather x2, waiting for transfers between devices, device_step(): all_normed = lax.all_gather(normed, 'dp', axis=0, tiled=True)  127 us
    all_gather x1, waiting for transfers between devices, device_step(): full_rows = lax.all_gather(residual, 'dp', axis=0, tiled=True)  53.5 us
    all_to_all x1, blocking collectives, device_step(): received = lax.all_to_all(part_sums, 'dp', 0, 0, tiled=True)  24.4 us
    unnamed x19, local copies, waits for them, and re-layouts  21.9 us
    dot_general x2, matrix products, mla_attention(): attn_out = jnp.dot(heads_out, w_o, preferred_element_type=jnp.float32)  17.2 us
    all_to_all x1, waiting for transfers between devices, device_step(): received = lax.all_to_all(part_sums, 'dp', 0, 0, tiled=True)  14.1 us
    dot_general x2, matrix products, mla_attention(): jnp.dot(q_low, wq_b, preferred_element_type=jnp.float32)  9.24 us
    dot_general x2, matrix products, mlp_partial(): return jnp.dot(activated, w_down, preferred_element_type=jnp.float32)  8.12 us
  transfers between devices with their start and end apart: 4, of which 4 were waited for; matrix products, arithmetic and copies ran while one was open for 3% of the time, Pallas kernels for 0%

commit v1 on v0

v1 whole, which is shorter than its diff:
```python
import functools

import jax
import jax.numpy as jnp
import numpy as np
from jax import lax
from jax.experimental import pallas as pl
from jax.experimental.pallas import tpu as pltpu
from jax.sharding import PartitionSpec as P

BF = jnp.bfloat16
F32 = jnp.float32
MESH = pl.DeviceIdType.MESH
NT = (((1,), (1,)), ((), ()))

SEQ = 1024
DIM = 2048
FFN = 10240
HEADS = 20
KVR = 512
NOPE = 192
ROPE = 64
QKD = NOPE + ROPE
CACHE = KVR + ROPE
QR = 768
VD = 256
ROWS = 2
PAD = 16
HP = 32
GROUP = 16
FS = FFN // GROUP
QB = 4
KC = 512
WOC = HEADS * VD // KC
AHEAD = 9


def rms(v, gain):
    return v * lax.rsqrt(jnp.mean(v * v, axis=-1, keepdims=True) + 1e-6) * gain


def rope_lanes(t, cos_t, sin_t):
    lane = lax.broadcasted_iota(jnp.int32, t.shape, 1)
    swapped = jnp.where(lane < ROPE // 2, pltpu.roll(t, 128 - ROPE // 2, 1), pltpu.roll(t, ROPE // 2, 1))
    return t * cos_t + swapped * sin_t


def attn_kernel(layer, len_ref, x_ref, freq_ref, ag_ref, kvg_ref, qg_ref, cache_ref, wdkv_ref, wqa_ref, wqb_ref, wuk_ref, wuv_ref, wo_ref,
                xo_ref, co_ref,
                wdkv, wqa, wqb, wuk, wuv, wo, cbuf, xs, ks, qf, qlat, qrs, of, ob, acc, sems, out_sem):
    half = HEADS // 2
    qc = HEADS * QKD // QB
    chunks = [(wdkv_ref.at[layer], wdkv), (wqa_ref.at[layer], wqa)]
    chunks += [(wqb_ref.at[layer, :, pl.ds(i * qc, qc)], wqb.at[:, pl.ds(i * qc, qc)]) for i in range(QB)]
    chunks += [(wuk_ref.at[layer, pl.ds(i * half, half)], wuk.at[pl.ds(i * half, half)]) for i in range(2)]
    chunks += [(cache_ref, cbuf)]
    chunks += [(wuv_ref.at[layer, pl.ds(i * half, half)], wuv.at[pl.ds(i * half, half)]) for i in range(2)]
    first_wo = len(chunks)
    chunks += [(wo_ref.at[layer, pl.ds(i * KC, KC)], wo.at[pl.ds(i * KC, KC)]) for i in range(WOC)]
    copies = [pltpu.make_async_copy(s, d, sems.at[i]) for i, (s, d) in enumerate(chunks)]
    for cp in copies[:AHEAD]:
        cp.start()

    def ready(i):
        copies[i].wait()
        if i + AHEAD < len(copies):
            copies[i + AHEAD].start()

    xs[...] = jnp.zeros_like(xs)
    xs[0:ROWS, :] = x_ref[...].astype(F32)
    ks[...] = jnp.zeros_like(ks)
    of[...] = jnp.zeros_like(of)
    for b in range(ROWS):
        qlat[b, 16:HP, :] = jnp.zeros((HP - 16, KVR), F32)
        qrs[b, 16:HP, :] = jnp.zeros((HP - 16, 128), F32)
    h = rms(xs[...], ag_ref[layer:layer + 1, :]).astype(BF)
    lane16 = lax.broadcasted_iota(jnp.int32, (PAD, 128), 1)
    row16 = lax.broadcasted_iota(jnp.int32, (PAD, 128), 0)
    angle = jnp.where(row16 == 0, len_ref[0], len_ref[1]).astype(F32) * freq_ref[...]
    cos_t = jnp.where(lane16 < ROPE, jnp.cos(angle), 0.0)
    sin_t = jnp.sin(angle)
    sin_t = jnp.where(lane16 < ROPE, jnp.where(lane16 < ROPE // 2, -sin_t, sin_t), 0.0)
    ready(0)
    k = lax.dot_general(h, wdkv[...], NT, preferred_element_type=F32)
    ready(1)
    qa = jnp.dot(h, wqa[...], preferred_element_type=F32)
    qa = rms(qa, qg_ref[layer:layer + 1, :]).astype(BF)
    ks[:, 0:CACHE] = k
    ks[:, 0:KVR] = rms(k[:, 0:KVR], kvg_ref[layer:layer + 1, :]).astype(BF).astype(F32)
    ks[:, KVR:KVR + 128] = rope_lanes(ks[:, KVR:KVR + 128], cos_t, sin_t).astype(BF).astype(F32)

    heads_q = HEADS // QB
    qparts = []
    for i in range(QB):
        ready(2 + i)
        qi = jnp.dot(qa, wqb[:, i * qc:(i + 1) * qc], preferred_element_type=F32).astype(BF)
        qf[:, i * qc:(i + 1) * qc] = qi.astype(F32)
        qparts.append(qi)
    for j in range(HEADS):
        if j % half == 0:
            ready(2 + QB + j // half)
        jj = j % heads_q
        qn = qparts[j // heads_q][:, jj * QKD:jj * QKD + NOPE]
        ql = jnp.dot(qn, wuk[j], preferred_element_type=F32)
        for b in range(ROWS):
            qlat[b, j:j + 1, :] = ql[b:b + 1, :]
            qrs[b, j:j + 1, :] = qf[b:b + 1, j * QKD + 128:(j + 1) * QKD]

    ready(4 + QB)
    ol = []
    outs = []
    ne = ks[:, 0:CACHE].astype(BF)
    for b in range(ROWS):
        p = len_ref[b]
        base = pl.multiple_of((p // 128) * 128, 128)
        hot = jnp.where((row16 == b) & (lane16 == p - base), 1.0, 0.0).astype(BF)
        col = lax.dot_general(ne, hot, (((0,), (0,)), ((), ())), preferred_element_type=F32)
        lane = lax.broadcasted_iota(jnp.int32, (CACHE, 128), 1)
        blk = cbuf[b, :, pl.ds(base, 128)].astype(F32)
        cbuf[b, :, pl.ds(base, 128)] = jnp.where(lane == p - base, col, blk).astype(BF)
    for b in range(ROWS):
        p = len_ref[b]
        qr = rope_lanes(pltpu.roll(qrs[b], 64, 1), cos_t[b:b + 1, :], sin_t[b:b + 1, :]).astype(BF)
        s = jnp.dot(qlat[b].astype(BF), cbuf[b, 0:KVR, :], preferred_element_type=F32)
        s += jnp.dot(qr[:, 0:ROPE], cbuf[b, KVR:CACHE, :], preferred_element_type=F32)
        s = s * (QKD ** -0.5)
        slot = lax.broadcasted_iota(jnp.int32, (HP, SEQ), 1)
        s = jnp.where(slot <= p, s, -1e30)
        e = jnp.exp(s - jnp.max(s, axis=-1, keepdims=True))
        a = (e / jnp.sum(e, axis=-1, keepdims=True)).astype(BF)
        ol.append(lax.dot_general(a, cbuf[b, 0:KVR, :], NT, preferred_element_type=F32).astype(BF))
        cp = pltpu.make_async_copy(cbuf.at[b], co_ref.at[b], out_sem.at[b])
        cp.start()
        outs.append(cp)
    olc = jnp.concatenate(ol, axis=0)
    for j in range(HEADS):
        if j % half == 0:
            ready(5 + QB + j // half)
        r = jnp.dot(olc, wuv[j], preferred_element_type=F32)
        for b in range(ROWS):
            of[b:b + 1, j * VD:(j + 1) * VD] = r[b * HP + j:b * HP + j + 1, :]
    for i in range(WOC):
        ob[i] = of[:, i * KC:(i + 1) * KC].astype(BF)
    acc[...] = jnp.zeros_like(acc)
    for i in range(first_wo, len(copies) - AHEAD):
        ready(i)
    late = max(first_wo, len(copies) - AHEAD)

    def step(i, carry):
        at = pl.ds(pl.multiple_of(i * KC, KC), KC)

        @pl.when(i >= late - first_wo)
        def _():
            pltpu.make_async_copy(wo_ref.at[layer, at], wo.at[at], sems.at[first_wo + i]).wait()

        acc[...] += jnp.dot(ob[i], wo[at, :], preferred_element_type=F32)
        return carry

    lax.fori_loop(0, WOC, step, 0)
    xo_ref[...] = (xs[0:ROWS, :] + acc[0:ROWS, :]).astype(BF)
    for cp in outs:
        cp.wait()


def attention(layer, lengths, x, freq, ag, kvg, qg, cache, wdkv, wqa, wqb, wuk, wuv, wo):
    vm = pl.BlockSpec(memory_space=pltpu.VMEM)
    anyspec = pl.BlockSpec(memory_space=pl.ANY)
    n_copies = 2 + QB + 2 + 1 + 2 + WOC
    wbytes = 2 * (DIM * CACHE + DIM * QR + QR * HEADS * QKD + HEADS * NOPE * KVR + HEADS * KVR * VD + HEADS * VD * DIM)
    return pl.pallas_call(
        functools.partial(attn_kernel, layer),
        out_shape=(jax.ShapeDtypeStruct((ROWS, DIM), BF), jax.ShapeDtypeStruct((ROWS, CACHE, SEQ), BF)),
        in_specs=[pl.BlockSpec(memory_space=pltpu.SMEM)] + [vm] * 5 + [anyspec] * 7,
        out_specs=(vm, anyspec),
        scratch_shapes=[
            pltpu.VMEM((CACHE, DIM), BF), pltpu.VMEM((DIM, QR), BF), pltpu.VMEM((QR, HEADS * QKD), BF),
            pltpu.VMEM((HEADS, NOPE, KVR), BF), pltpu.VMEM((HEADS, KVR, VD), BF), pltpu.VMEM((HEADS * VD, DIM), BF),
            pltpu.VMEM((ROWS, CACHE, SEQ), BF), pltpu.VMEM((PAD, DIM), F32), pltpu.VMEM((PAD, KVR + 128), F32),
            pltpu.VMEM((PAD, HEADS * QKD), F32), pltpu.VMEM((ROWS, HP, KVR), F32), pltpu.VMEM((ROWS, HP, 128), F32),
            pltpu.VMEM((PAD, HEADS * VD), F32), pltpu.VMEM((WOC, PAD, KC), BF), pltpu.VMEM((PAD, DIM), F32),
            pltpu.SemaphoreType.DMA((n_copies,)), pltpu.SemaphoreType.DMA((ROWS,)),
        ],
        compiler_params=pltpu.CompilerParams(vmem_limit_bytes=62 * 1024 * 1024),
        cost_estimate=pl.CostEstimate(flops=wbytes * 2, bytes_accessed=wbytes, transcendentals=0),
        name=f"attn{layer}",
    )(lengths, x, freq, ag, kvg, qg, cache, wdkv, wqa, wqb, wuk, wuv, wo)


def dev(i):
    return (lax.axis_index("replica"), i)


def remote(src, dst, send_sem, recv_sem, peer):
    return pltpu.make_async_remote_copy(src_ref=src, dst_ref=dst, send_sem=send_sem, recv_sem=recv_sem, device_id=dev(peer), device_id_type=MESH)


def mlp_kernel(layer, final, x_ref, gain_ref, wg_ref, wu_ref, wd_ref, out_ref, xg, xf, wg, wu, wd, pf, ps, pr, fb, wsem, s1, r1, s2, r2, fs, fr, os_):
    idx = lax.axis_index("dp")
    me = lax.rem(idx, GROUP)
    first = idx - me
    core = lax.rem(idx, 2)
    cx = lax.rem(lax.div(idx, 2), 4)
    cy = lax.rem(lax.div(idx, 8), 4)
    cz = lax.div(idx, 32)
    at = pl.ds(pl.multiple_of(me * FS, FS), FS)
    loads = [pltpu.make_async_copy(wg_ref.at[layer, :, at], wg, wsem.at[0]),
             pltpu.make_async_copy(wu_ref.at[layer, :, at], wu, wsem.at[1]),
             pltpu.make_async_copy(wd_ref.at[layer, at, :], wd, wsem.at[2])]
    for cp in loads:
        cp.start()

    def rank(k):
        return lax.rem(me + k, GROUP)

    peers = [first + rank(k) for k in range(1, GROUP)]
    if final:
        other = lax.rem(lax.div(cy, 2) + 1, 2) * 2
        peers += [cz * 32 + (other + k) * 8 + cx * 2 + core for k in range(2)]
        peers += [lax.rem(cz + k, 4) * 32 + cy * 8 + cx * 2 + core for k in range(1, 4)]
    barrier = pltpu.get_barrier_semaphore()
    for p in peers:
        pl.semaphore_signal(barrier, inc=1, device_id=dev(p), device_id_type=MESH)
    pl.semaphore_wait(barrier, len(peers))

    order = sorted(range(1, GROUP), key=lambda k: -min(k, GROUP - k))
    sends = {}
    for k in order:
        sends[k] = remote(x_ref, xg.at[me], s1.at[k], r1.at[k], first + rank(k))
        sends[k].start()
    xg[me] = x_ref[...]
    for k in range(1, GROUP):
        src = rank(GROUP - k)
        remote(x_ref, xg.at[src], s1.at[k], r1.at[k], first + src).wait_recv()
    for d in range(GROUP):
        xf[ROWS * d:ROWS * (d + 1), :] = xg[d].astype(F32)
    g = rms(xf[...], gain_ref[layer:layer + 1, :]).astype(BF)
    loads[0].wait()
    gate = jnp.dot(g, wg[...], preferred_element_type=F32)
    loads[1].wait()
    up = jnp.dot(g, wu[...], preferred_element_type=F32)
    u = (gate * jax.nn.sigmoid(gate) * up).astype(BF)
    loads[2].wait()
    pf[...] = jnp.dot(u, wd[...], preferred_element_type=F32)
    for d in range(GROUP):
        ps[d] = pf[ROWS * d:ROWS * (d + 1), :].astype(BF)
    back = {}
    for k in order:
        dst = rank(k)
        back[k] = remote(ps.at[dst], pr.at[me], s2.at[k], r2.at[k], first + dst)
        back[k].start()
    pr[me] = ps[me]
    for k in range(1, GROUP):
        src = rank(GROUP - k)
        remote(ps.at[src], pr.at[src], s2.at[k], r2.at[k], first + src).wait_recv()
    total = pr[0].astype(F32)
    for d in range(1, GROUP):
        total += pr[d].astype(F32)
    fin = (x_ref[...].astype(F32) + total).astype(BF)
    if not final:
        out_ref[...] = fin
    else:
        fb[core, cz, cy, cx] = fin
        partner = idx + 1 - 2 * core
        started = []

        def stage(n, slot_of, peer_of):
            for k in range(1, 4):
                cp = remote(slot_of(0), slot_of(0), fs.at[n, k], fr.at[n, k], peer_of(k))
                cp.start()
                started.append(cp)
            return [remote(slot_of(4 - k), slot_of(4 - k), fs.at[n, k], fr.at[n, k], peer_of(4 - k)) for k in range(1, 4)]

        def xs(k):
            return fb.at[core, cz, cy, lax.rem(cx + k, 4)]

        def ys(k):
            return fb.at[core, cz, lax.rem(cy + k, 4)]

        def zs(k):
            return fb.at[core, lax.rem(cz + k, 4)]

        for cp in stage(0, xs, lambda k: cz * 32 + cy * 8 + lax.rem(cx + k, 4) * 2 + core):
            cp.wait_recv()
        for cp in stage(1, ys, lambda k: cz * 32 + lax.rem(cy + k, 4) * 8 + cx * 2 + core):
            cp.wait_recv()
        arrivals = stage(2, zs, lambda k: lax.rem(cz + k, 4) * 32 + cy * 8 + cx * 2 + core)
        outs = []

        def put(c, z, n):
            cp = pltpu.make_async_copy(fb.at[c, z], out_ref.at[z, :, :, c], os_.at[n])
            cp.start()
            outs.append(cp)

        def share(k):
            z = lax.rem(cz + k, 4)
            cp = remote(fb.at[core, z], fb.at[core, z], fs.at[3, k], fr.at[3, k], partner)
            cp.start()
            started.append(cp)
            put(core, z, k)

        share(0)
        for k in range(1, 4):
            arrivals[k - 1].wait_recv()
            share(4 - k)
        for k in (0, 3, 2, 1):
            z = lax.rem(cz + k, 4)
            remote(fb.at[1 - core, z], fb.at[1 - core, z], fs.at[3, k], fr.at[3, k], partner).wait_recv()
            put(1 - core, z, 4 + k)
        for cp in started:
            cp.wait_send()
        for cp in outs:
            cp.wait()
    for k in order:
        sends[k].wait_send()
        back[k].wait_send()


def mlp(layer, final, x, gain, wg, wu, wd):
    vm = pl.BlockSpec(memory_space=pltpu.VMEM)
    anyspec = pl.BlockSpec(memory_space=pl.ANY)
    out = jax.ShapeDtypeStruct((4, 4, 4, 2, ROWS, DIM) if final else (ROWS, DIM), BF)
    dma = pltpu.SemaphoreType.DMA
    return pl.pallas_call(
        functools.partial(mlp_kernel, layer, final),
        out_shape=out,
        in_specs=[vm, vm, anyspec, anyspec, anyspec],
        out_specs=anyspec if final else vm,
        scratch_shapes=[
            pltpu.VMEM((GROUP, ROWS, DIM), BF), pltpu.VMEM((GROUP * ROWS, DIM), F32),
            pltpu.VMEM((DIM, FS), BF), pltpu.VMEM((DIM, FS), BF), pltpu.VMEM((FS, DIM), BF),
            pltpu.VMEM((GROUP * ROWS, DIM), F32), pltpu.VMEM((GROUP, ROWS, DIM), BF), pltpu.VMEM((GROUP, ROWS, DIM), BF),
            pltpu.VMEM((2, 4, 4, 4, ROWS, DIM) if final else (1, ROWS, DIM), BF),
            dma((3,)), dma((GROUP,)), dma((GROUP,)), dma((GROUP,)), dma((GROUP,)), dma((4, 4)), dma((4, 4)), dma((8,)),
        ],
        compiler_params=pltpu.CompilerParams(vmem_limit_bytes=32 * 1024 * 1024, collective_id=layer, has_side_effects=True),
        cost_estimate=pl.CostEstimate(flops=200000000, bytes_accessed=8000000, transcendentals=0),
        name=f"mlp{layer}",
    )(x, gain, wg, wu, wd)


def solution(mesh):
    row_spec = P(("replica", "dp"), None)
    len_spec = P(("replica", "dp"))
    cache_spec = P(("replica", "dp"), None, None)
    in_specs = (row_spec, len_spec, cache_spec, cache_spec) + (P(),) * 13
    out_specs = (P("replica", None), cache_spec, cache_spec)

    def device_step(x_rows, lengths, cache0, cache1, attn_gain, w_dkv, kv_gain, wq_a, q_gain, wq_b, w_uk, w_uv, w_o, ffn_gain, w_gate, w_up, w_down):
        half = ROPE // 2
        inv_freq = 10000.0 ** (-(np.arange(128) % half) / half)
        freq = jnp.asarray(inv_freq[None, :], F32)
        w_dkv = w_dkv.transpose(0, 2, 1)
        x = x_rows
        caches = []
        for layer, cache in enumerate((cache0, cache1)):
            x, c = attention(layer, lengths, x, freq, attn_gain, kv_gain, q_gain, cache.transpose(0, 2, 1), w_dkv, wq_a, wq_b, w_uk, w_uv, w_o)
            caches.append(c.transpose(0, 2, 1))
            x = mlp(layer, layer == 1, x, ffn_gain, w_gate, w_up, w_down)
        return x.reshape(-1, DIM), caches[0], caches[1]

    return jax.shard_map(device_step, mesh=mesh, in_specs=in_specs, out_specs=out_specs, check_vma=False)
```

time: 345 us -> 88.1 us (0.26)
  waiting for transfers between devices: 195 us -> 0 us
  Pallas kernels: 0 us -> 83.9 us
  matrix products: 62.9 us -> 0 us
  local copies, waits for them, and re-layouts: 29.3 us -> 3.2 us
  blocking collectives: 24.4 us -> 0 us
  between operations: 13.9 us -> 0.7 us
  other arithmetic: 11.6 us -> 0 us
  starting transfers between devices: 6.14 us -> 0 us
    all_gather x3 -> x0, waiting for transfers between devices: 181 us -> none  [the longest x2 127 us: device_step(): all_normed = lax.all_gather(normed, 'dp', axis=0, tiled=True)]
    pallas_call x0 -> x4, Pallas kernels: none -> 83.9 us  [the longest x2 49.4 us: mlp(): pl.pallas_call(functools.partial(mlp_kernel, layer, final), out_shape=out...]
    dot_general x20 -> x0, matrix products: 62.9 us -> none  [the longest x2 17.2 us: mla_attention(): attn_out = jnp.dot(heads_out, w_o, preferred_element_type=jnp.float32)]
    all_to_all x1 -> x0, blocking collectives: 24.4 us -> none  [device_step(): received = lax.all_to_all(part_sums, 'dp', 0, 0, tiled=True)]
    unnamed x19 -> x8, local copies, waits for them, and re-layouts: 21.9 us -> 1.98 us
    all_to_all x1 -> x0, waiting for transfers between devices: 14.1 us -> none  [device_step(): received = lax.all_to_all(part_sums, 'dp', 0, 0, tiled=True)]
    all_to_all x1 -> x0, starting transfers between devices: 5.83 us -> none  [device_step(): received = lax.all_to_all(part_sums, 'dp', 0, 0, tiled=True)]
    all_to_all x2 -> x0, local copies, waits for them, and re-layouts: 5.05 us -> none  [device_step(): received = lax.all_to_all(part_sums, 'dp', 0, 0, tiled=True)]
  transfers between devices with their start and end apart: 4 -> 0, of which waited for: 4 -> 0; matrix products, arithmetic and copies ran while one was open for 3% -> 0% of each run, Pallas kernels for 0% -> 0%
where the time goes in v1:
time: 88.1 us; the launch traced here: 87.8 us
  Pallas kernels  83.9 us (95%)
  local copies, waits for them, and re-layouts  3.2 us (4%)
    pallas_call x2, Pallas kernels, mlp(): pl.pallas_call(functools.partial(mlp_kernel, layer, final), out_shape=out...  49.4 us
    pallas_call x2, Pallas kernels, attention(): pl.pallas_call(functools.partial(attn_kernel, layer), out_shape=(jax.Shap...  34.5 us
    unnamed x8, local copies, waits for them, and re-layouts  1.98 us

profile of v1, /device:TPU:1, one launch (start us, length us, event | category | flops | bytes accessed | tf_op | source)
XLA Modules:
  0.0 87.8 jit_solution(13089584028093195743)
XLA Ops:
  0.6 0.0 copy-start
  0.6 17.3 %attn0.1 = (bf16[2,2048]{1,0:T(2,128)(2,1)}, bf16[2,576,1024]{2,1,0:T(8,128)(2,1)}) custom-call(s32[2]{0:T(128)} %len_ref.3, bf16[2,2048]{1,0:T(2,128)(2,1)} %x_ref.1, f32[1,128]{1,0:T(1,128)} %constant.2.clone.freq_ref, f32[2,2048]{1,0:T(2,128)} %ag_ref.3, f32[2,512]{1,0:T(2,128)} %kvg_ref.3, f32[2,768]{1,0:T(2,128)} %qg_ref.3, ...), custom_call_target="tpu_custom_call" | custom-call | flops 87031808 | bytes 43515904 | tf_op jit(solution)/shard_map/attn0/pallas_call | solution.py:170
  17.9 0.0 copy-done
  17.9 0.0 copy-start.3
  17.9 0.7 copy-done.3
  18.6 16.5 %mlp0.1.x_ref = bf16[2,2048]{1,0:T(2,128)(2,1)S(1)} custom-call(bf16[2,2048]{1,0:T(2,128)(2,1)S(1)} %copy-done.3, f32[2,2048]{1,0:T(2,128)S(1)} %copy-done, bf16[2,2048,10240]{2,1,0:T(8,128)(2,1)} %wg_ref.3, bf16[2,2048,10240]{2,1,0:T(8,128)(2,1)} %wu_ref.3, bf16[2,10240,2048]{2,1,0:T(8,128)(2,1)} %wd_ref.3), custom_call_target="tpu_custom_call" | custom-call | flops 200000000 | bytes 8000000 | tf_op jit(solution)/shard_map/mlp0/pallas_call | solution.py:323
  35.1 0.0 copy-start.1
  35.1 0.6 copy-done.1
  35.7 17.2 %attn1.1 = (bf16[2,2048]{1,0:T(2,128)(2,1)}, bf16[2,576,1024]{2,1,0:T(8,128)(2,1)}) custom-call(s32[2]{0:T(128)} %len_ref.3, bf16[2,2048]{1,0:T(2,128)(2,1)} %copy-done.1, f32[1,128]{1,0:T(1,128)} %constant.2.clone.freq_ref, f32[2,2048]{1,0:T(2,128)} %ag_ref.3, f32[2,512]{1,0:T(2,128)} %kvg_ref.3, f32[2,768]{1,0:T(2,128)} %qg_ref.3, ...), custom_call_target="tpu_custom_call" | custom-call | flops 87031808 | bytes 43515904 | tf_op jit(solution)/shard_map/attn1/pallas_call | solution.py:170
  53.0 0.0 copy-start.2
  53.0 0.7 copy-done.2
  53.7 32.9 %mlp1.1 = bf16[4,4,4,2,2,2048]{5,4,3,2,1,0:T(2,128)(2,1)S(1)} custom-call(bf16[2,2048]{1,0:T(2,128)(2,1)S(1)} %copy-done.2, f32[2,2048]{1,0:T(2,128)S(1)} %copy-done, bf16[2,2048,10240]{2,1,0:T(8,128)(2,1)} %wg_ref.3, bf16[2,2048,10240]{2,1,0:T(8,128)(2,1)} %wu_ref.3, bf16[2,10240,2048]{2,1,0:T(8,128)(2,1)} %wd_ref.3), custom_call_target="tpu_custom_call" | custom-call | flops 200000000 | bytes 8000000 | tf_op jit(solution)/shard_map/mlp1/pallas_call | solution.py:323
  86.6 1.2 %reshape.9 = bf16[256,2048]{1,0:T(8,128)(2,1)} reshape(bf16[4,4,4,2,2,2048]{5,4,3,2,1,0:T(2,128)(2,1)S(1)} %mlp1.1) | data formatting | bytes 2097152 | tf_op jit(solution)/shard_map/reshape | solution.py:359
Async XLA Ops:
  0.6 17.3 %copy-start = (f32[2,2048]{1,0:T(2,128)S(1)}, f32[2,2048]{1,0:T(2,128)}, u32[]{:S(2)}) copy-start(f32[2,2048]{1,0:T(2,128)} %gain_ref.3) | copy-start | bytes 49156
  17.9 0.7 copy-start.3
  35.1 0.6 copy-start.1
  53.0 0.7 copy-start.2

commit v2 on v0

v2 whole, which is shorter than its diff:
```python
import functools

import jax
import jax.numpy as jnp
import numpy as np
from jax import lax
from jax.experimental import pallas as pl
from jax.experimental.pallas import tpu as pltpu
from jax.sharding import PartitionSpec as P

BF = jnp.bfloat16
F32 = jnp.float32
MESH = pl.DeviceIdType.MESH
NT = (((1,), (1,)), ((), ()))

SEQ = 1024
DIM = 2048
FFN = 10240
HEADS = 20
KVR = 512
NOPE = 192
ROPE = 64
QKD = NOPE + ROPE
CACHE = KVR + ROPE
QR = 768
VD = 256
ROWS = 2
PAD = 16
HP = 32
GROUP = 16
FS = FFN // GROUP
QB = 4
KC = 512
WOC = HEADS * VD // KC
AHEAD = 13


def rms(v, gain):
    return v * lax.rsqrt(jnp.mean(v * v, axis=-1, keepdims=True) + 1e-6) * gain


def rope_lanes(t, cos_t, sin_t):
    lane = lax.broadcasted_iota(jnp.int32, t.shape, 1)
    swapped = jnp.where(lane < ROPE // 2, pltpu.roll(t, 128 - ROPE // 2, 1), pltpu.roll(t, ROPE // 2, 1))
    return t * cos_t + swapped * sin_t


def dev(i):
    return (lax.axis_index("replica"), i)


def remote(src, dst, send_sem, recv_sem, peer):
    return pltpu.make_async_remote_copy(src_ref=src, dst_ref=dst, send_sem=send_sem, recv_sem=recv_sem, device_id=dev(peer), device_id_type=MESH)


def step_kernel(len_ref, x_ref, freq_ref, ag_ref, kvg_ref, qg_ref, fg_ref, cache0_ref, cache1_ref, wdkv_ref, wqa_ref, wqb_ref, wuk_ref, wuv_ref, wo_ref, wg_ref, wu_ref, wd_ref,
                out_ref, ne_ref,
                wdkv, wqa, wqb, wuk, wuv, wo, cbuf, wg, wu, wd, xs, ks, qf, qlat, qrs, of, ob, acc, xm, xg, xf, pf, ps, pr, ps2, pr2, fb,
                sems, s1, r1, s2, r2, fs, fr, ds, dr, os_):
    idx = lax.axis_index("dp")
    core = lax.rem(idx, 2)
    cx = lax.rem(lax.div(idx, 2), 4)
    cy = lax.rem(lax.div(idx, 8), 4)
    cz = lax.div(idx, 32)
    gx, gy, gz = lax.div(cx, 2), lax.div(cy, 2), lax.div(cz, 2)
    bx, by, bz = lax.rem(cx, 2), lax.rem(cy, 2), lax.rem(cz, 2)
    chip = bz * 4 + by * 2 + bx
    me = chip * 2 + core

    def index(z, y, x, c):
        return z * 32 + y * 8 + x * 2 + c

    def flip(m):
        z = lax.rem(bz + m // 8, 2)
        y = lax.rem(by + m // 4 % 2, 2)
        x = lax.rem(bx + m // 2 % 2, 2)
        c = lax.rem(core + m % 2, 2)
        return z * 8 + y * 4 + x * 2 + c, index(gz * 2 + z, gy * 2 + y, gx * 2 + x, c)

    def away(k):
        return index(lax.rem(cz + lax.div(k, 16), 4), lax.rem(cy + lax.rem(lax.div(k, 4), 4), 4), lax.rem(cx + lax.rem(k, 4), 4), core)

    barrier = pltpu.get_barrier_semaphore()

    def greet(k, carry):
        pl.semaphore_signal(barrier, inc=1, device_id=dev(away(k)), device_id_type=MESH)
        return carry

    lax.fori_loop(1, 64, greet, 0)
    for m in range(1, GROUP, 2):
        pl.semaphore_signal(barrier, inc=1, device_id=dev(flip(m)[1]), device_id_type=MESH)

    half = HEADS // 2
    qc = HEADS * QKD // QB
    mine = pl.ds(pl.multiple_of(me * FS, FS), FS)

    def loads_of(layer):
        chunks = [(wdkv_ref.at[layer], wdkv), (wqa_ref.at[layer], wqa)]
        chunks += [(wqb_ref.at[layer, :, pl.ds(i * qc, qc)], wqb.at[:, pl.ds(i * qc, qc)]) for i in range(QB)]
        chunks += [(wuk_ref.at[layer, pl.ds(i * half, half)], wuk.at[pl.ds(i * half, half)]) for i in range(2)]
        chunks += [((cache0_ref, cache1_ref)[layer], cbuf)]
        chunks += [(wuv_ref.at[layer, pl.ds(i * half, half)], wuv.at[pl.ds(i * half, half)]) for i in range(2)]
        chunks += [(wo_ref.at[layer, pl.ds(i * KC, KC)], wo.at[pl.ds(i * KC, KC)]) for i in range(WOC)]
        chunks += [(wg_ref.at[layer, :, mine], wg), (wu_ref.at[layer, :, mine], wu), (wd_ref.at[layer, mine, :], wd)]
        return [pltpu.make_async_copy(s, d, sems.at[i]) for i, (s, d) in enumerate(chunks)]

    first_uv = 5 + QB
    first_wo = first_uv + 2
    first_mlp = first_wo + WOC
    loads = [loads_of(0), loads_of(1)]
    for cp in loads[0][:AHEAD]:
        cp.start()

    lane16 = lax.broadcasted_iota(jnp.int32, (PAD, 128), 1)
    row16 = lax.broadcasted_iota(jnp.int32, (PAD, 128), 0)
    angle = jnp.where(row16 == 0, len_ref[0], len_ref[1]).astype(F32) * freq_ref[...]
    cos_t = jnp.where(lane16 < ROPE, jnp.cos(angle), 0.0)
    sin_t = jnp.sin(angle)
    sin_t = jnp.where(lane16 < ROPE, jnp.where(lane16 < ROPE // 2, -sin_t, sin_t), 0.0)

    xs[...] = jnp.zeros_like(xs)
    xs[0:ROWS, :] = x_ref[...].astype(F32)
    ks[...] = jnp.zeros_like(ks)
    of[...] = jnp.zeros_like(of)
    for b in range(ROWS):
        qlat[b, 16:HP, :] = jnp.zeros((HP - 16, KVR), F32)
        qrs[b, 16:HP, :] = jnp.zeros((HP - 16, 128), F32)

    def attention(layer):
        def ready(i):
            loads[layer][i].wait()
            if layer == 0 and i + AHEAD < len(loads[0]):
                loads[0][i + AHEAD].start()

        h = rms(xs[...], ag_ref[layer:layer + 1, :]).astype(BF)
        ready(0)
        k = lax.dot_general(h, wdkv[...], NT, preferred_element_type=F32)
        ready(1)
        qa = jnp.dot(h, wqa[...], preferred_element_type=F32)
        qa = rms(qa, qg_ref[layer:layer + 1, :]).astype(BF)
        ks[:, 0:CACHE] = k
        ks[:, 0:KVR] = rms(k[:, 0:KVR], kvg_ref[layer:layer + 1, :]).astype(BF).astype(F32)
        ks[:, KVR:KVR + 128] = rope_lanes(ks[:, KVR:KVR + 128], cos_t, sin_t).astype(BF).astype(F32)
        ne_ref[layer] = ks[0:ROWS, 0:CACHE].astype(BF)

        heads_q = HEADS // QB
        qparts = []
        for i in range(QB):
            ready(2 + i)
            qi = jnp.dot(qa, wqb[:, i * qc:(i + 1) * qc], preferred_element_type=F32).astype(BF)
            qf[:, i * qc:(i + 1) * qc] = qi.astype(F32)
            qparts.append(qi)
        for j in range(HEADS):
            if j % half == 0:
                ready(2 + QB + j // half)
            jj = j % heads_q
            qn = qparts[j // heads_q][:, jj * QKD:jj * QKD + NOPE]
            ql = jnp.dot(qn, wuk[j], preferred_element_type=F32)
            for b in range(ROWS):
                qlat[b, j:j + 1, :] = ql[b:b + 1, :]
                qrs[b, j:j + 1, :] = qf[b:b + 1, j * QKD + 128:(j + 1) * QKD]

        ready(4 + QB)
        ol = []
        slot = lax.broadcasted_iota(jnp.int32, (HP, SEQ), 1)
        for b in range(ROWS):
            p = len_ref[b]
            ql = qlat[b].astype(BF)
            qr = rope_lanes(pltpu.roll(qrs[b], 64, 1), cos_t[b:b + 1, :], sin_t[b:b + 1, :]).astype(BF)
            s = jnp.dot(ql, cbuf[b, 0:KVR, :], preferred_element_type=F32)
            s += jnp.dot(qr[:, 0:ROPE], cbuf[b, KVR:CACHE, :], preferred_element_type=F32)
            own = jnp.sum(ql.astype(F32) * ks[b:b + 1, 0:KVR], axis=-1, keepdims=True)
            own += jnp.sum(qr.astype(F32) * ks[b:b + 1, KVR:KVR + 128], axis=-1, keepdims=True)
            s = jnp.where(slot == p, own, s) * (QKD ** -0.5)
            s = jnp.where(slot <= p, s, -1e30)
            e = jnp.exp(s - jnp.max(s, axis=-1, keepdims=True))
            a = (e / jnp.sum(e, axis=-1, keepdims=True)).astype(BF)
            af = a.astype(F32)
            a_own = jnp.sum(jnp.where(slot == p, af, 0.0), axis=-1, keepdims=True)
            a_old = jnp.where(slot == p, 0.0, af).astype(BF)
            o = lax.dot_general(a_old, cbuf[b, 0:KVR, :], NT, preferred_element_type=F32)
            ol.append((o + a_own * ks[b:b + 1, 0:KVR]).astype(BF))
        olc = jnp.concatenate(ol, axis=0)
        for j in range(HEADS):
            if j % half == 0:
                ready(first_uv + j // half)
            r = jnp.dot(olc, wuv[j], preferred_element_type=F32)
            for b in range(ROWS):
                of[b:b + 1, j * VD:(j + 1) * VD] = r[b * HP + j:b * HP + j + 1, :]
        for i in range(WOC):
            ob[i] = of[:, i * KC:(i + 1) * KC].astype(BF)
        acc[...] = jnp.zeros_like(acc)

        def step(i, carry):
            at = pl.ds(pl.multiple_of(i * KC, KC), KC)
            pltpu.make_async_copy(wo_ref.at[layer, at], wo.at[at], sems.at[first_wo + i]).wait()
            acc[...] += jnp.dot(ob[i], wo[at, :], preferred_element_type=F32)
            return carry

        lax.fori_loop(0, WOC, step, 0)
        xm[layer] = (xs[0:ROWS, :] + acc[0:ROWS, :]).astype(BF)

    def group_rows(layer):
        copies = []
        for m in range(GROUP - 1, 0, -1):
            cp = remote(xm.at[layer], xg.at[me], s1.at[layer, m], r1.at[layer, m], flip(m)[1])
            cp.start()
            copies.append(cp)
        return copies

    def mlp_share(layer):
        xg[me] = xm[layer]
        for m in range(1, GROUP):
            r, peer = flip(m)
            remote(xm.at[layer], xg.at[r], s1.at[layer, m], r1.at[layer, m], peer).wait_recv()
        for d in range(GROUP):
            xf[ROWS * d:ROWS * (d + 1), :] = xg[d].astype(F32)
        g = rms(xf[...], fg_ref[layer:layer + 1, :]).astype(BF)
        loads[layer][first_mlp].wait()
        gate = jnp.dot(g, wg[...], preferred_element_type=F32)
        loads[layer][first_mlp + 1].wait()
        up = jnp.dot(g, wu[...], preferred_element_type=F32)
        u = (gate * jax.nn.sigmoid(gate) * up).astype(BF)
        loads[layer][first_mlp + 2].wait()
        pf[...] = jnp.dot(u, wd[...], preferred_element_type=F32)

    attention(0)
    pl.semaphore_wait(barrier, 63 + GROUP // 2)
    sent = group_rows(0)
    for cp in loads[1][:4 + QB]:
        cp.start()
    mlp_share(0)
    for d in range(GROUP):
        ps[d] = pf[ROWS * d:ROWS * (d + 1), :].astype(BF)
    for m in range(GROUP - 1, 0, -1):
        r, peer = flip(m)
        cp = remote(ps.at[r], pr.at[me], s2.at[0, m], r2.at[0, m], peer)
        cp.start()
        sent.append(cp)
    for cp in loads[1][4 + QB:]:
        cp.start()
    pr[me] = ps[me]
    for m in range(1, GROUP):
        r, peer = flip(m)
        remote(ps.at[r], pr.at[r], s2.at[0, m], r2.at[0, m], peer).wait_recv()
    total = pr[0].astype(F32)
    for d in range(1, GROUP):
        total += pr[d].astype(F32)
    xs[0:ROWS, :] = (xm[0].astype(F32) + total).astype(BF).astype(F32)

    attention(1)
    sent += group_rows(1)
    mlp_share(1)
    def cols(q, c):
        return pl.ds(pl.multiple_of(c * 1024 + q * 128, 128), 128)

    for d in range(GROUP):
        ps2[d] = pf[:, (d % 2) * 1024 + d // 2 * 128:(d % 2) * 1024 + d // 2 * 128 + 128].astype(BF)
    for m in range(GROUP - 1, 0, -1):
        r, peer = flip(m)
        cp = remote(ps2.at[r], pr2.at[me], s2.at[1, m], r2.at[1, m], peer)
        cp.start()
        sent.append(cp)
    pr2[me] = ps2[me]
    for m in range(1, GROUP):
        r, peer = flip(m)
        remote(ps2.at[r], pr2.at[r], s2.at[1, m], r2.at[1, m], peer).wait_recv()
    total = pr2[0].astype(F32)
    for d in range(1, GROUP):
        total += pr2[d].astype(F32)
    fin = (xf[:, cols(chip, core)] + total).astype(BF)
    for z in range(2):
        for y in range(2):
            fb[gz * 2 + z, gy * 2 + y, gx, :, cols(chip, core)] = fin[(z * 2 + y) * 8:(z * 2 + y) * 8 + 8, :]

    def block(ref, z, y, x, c):
        q = lax.rem(z, 2) * 4 + lax.rem(y, 2) * 2 + lax.rem(x, 2)
        return ref.at[pl.ds(lax.div(z, 2) * 2, 2), pl.ds(lax.div(y, 2) * 2, 2), lax.div(x, 2), :, cols(q, c)]

    def side(ref, z, y, x, c):
        return ref.at[pl.ds(z * 2, 2), pl.ds(y * 2, 2), x, :, pl.ds(pl.multiple_of(c * 1024, 1024), 1024)]

    own_block = block(fb, cz, cy, cx, core)

    def digit(a):
        return lax.rem(2 + 3 * a, 4)

    def spread(i, carry):
        k = digit(lax.div(i, 16)) * 16 + digit(lax.rem(lax.div(i, 4), 4)) * 4 + digit(lax.rem(i, 4))

        @pl.when(k != 0)
        def _():
            remote(own_block, own_block, fs.at[k], fr.at[k], away(k)).start()
        return carry

    lax.fori_loop(0, 64, spread, 0)
    partner = index(cz, cy, cx, 1 - core)

    def gathered(t, carry):
        z = lax.rem(gz + lax.div(t, 4), 2)
        y = lax.rem(gy + lax.rem(lax.div(t, 2), 2), 2)
        x = lax.rem(gx + lax.rem(t, 2), 2)

        def arrive(q, carry):
            oz, oy, ox = z * 2 + lax.div(q, 4), y * 2 + lax.rem(lax.div(q, 2), 2), x * 2 + lax.rem(q, 2)
            k = lax.rem(cz + 4 - oz, 4) * 16 + lax.rem(cy + 4 - oy, 4) * 4 + lax.rem(cx + 4 - ox, 4)

            @pl.when(k != 0)
            def _():
                remote(own_block, block(fb, oz, oy, ox, core), fs.at[k], fr.at[k], index(oz, oy, ox, core)).wait_recv()
            return carry

        lax.fori_loop(0, 8, arrive, 0)
        part = side(fb, z, y, x, core)
        remote(part, part, ds.at[t], dr.at[t], partner).start()
        pltpu.make_async_copy(part, side(out_ref, z, y, x, core), os_.at[t]).start()
        return carry

    lax.fori_loop(0, 8, gathered, 0)

    def passed(t, carry):
        z = lax.rem(gz + lax.div(t, 4), 2)
        y = lax.rem(gy + lax.rem(lax.div(t, 2), 2), 2)
        x = lax.rem(gx + lax.rem(t, 2), 2)
        part = side(fb, z, y, x, 1 - core)
        remote(part, part, ds.at[t], dr.at[t], partner).wait_recv()
        pltpu.make_async_copy(part, side(out_ref, z, y, x, 1 - core), os_.at[8 + t]).start()
        return carry

    lax.fori_loop(0, 8, passed, 0)
    for cp in sent:
        cp.wait_send()

    def sent_block(k, carry):
        remote(own_block, own_block, fs.at[k], fr.at[k], away(k)).wait_send()
        return carry

    lax.fori_loop(1, 64, sent_block, 0)

    def finish(t, carry):
        part = side(fb, 0, 0, 0, core)
        remote(part, part, ds.at[t], dr.at[t], partner).wait_send()
        pltpu.make_async_copy(part, side(out_ref, 0, 0, 0, core), os_.at[t]).wait()
        pltpu.make_async_copy(part, side(out_ref, 0, 0, 0, core), os_.at[8 + t]).wait()
        return carry

    lax.fori_loop(0, 8, finish, 0)


def two_layers(lengths, x, freq, ag, kvg, qg, fg, cache0, cache1, wdkv, wqa, wqb, wuk, wuv, wo, wg, wu, wd):
    vm = pl.BlockSpec(memory_space=pltpu.VMEM)
    anyspec = pl.BlockSpec(memory_space=pl.ANY)
    dma = pltpu.SemaphoreType.DMA
    n_loads = 5 + QB + 2 + WOC + 3
    return pl.pallas_call(
        step_kernel,
        out_shape=(jax.ShapeDtypeStruct((4, 4, 2, 8, DIM), BF), jax.ShapeDtypeStruct((2, ROWS, CACHE), BF)),
        in_specs=[pl.BlockSpec(memory_space=pltpu.SMEM)] + [vm] * 6 + [anyspec] * 11,
        out_specs=(anyspec, vm),
        scratch_shapes=[
            pltpu.VMEM((CACHE, DIM), BF), pltpu.VMEM((DIM, QR), BF), pltpu.VMEM((QR, HEADS * QKD), BF),
            pltpu.VMEM((HEADS, NOPE, KVR), BF), pltpu.VMEM((HEADS, KVR, VD), BF), pltpu.VMEM((HEADS * VD, DIM), BF),
            pltpu.VMEM((ROWS, CACHE, SEQ), BF),
            pltpu.VMEM((DIM, FS), BF), pltpu.VMEM((DIM, FS), BF), pltpu.VMEM((FS, DIM), BF),
            pltpu.VMEM((PAD, DIM), F32), pltpu.VMEM((PAD, KVR + 128), F32),
            pltpu.VMEM((PAD, HEADS * QKD), F32), pltpu.VMEM((ROWS, HP, KVR), F32), pltpu.VMEM((ROWS, HP, 128), F32),
            pltpu.VMEM((PAD, HEADS * VD), F32), pltpu.VMEM((WOC, PAD, KC), BF), pltpu.VMEM((PAD, DIM), F32),
            pltpu.VMEM((2, ROWS, DIM), BF), pltpu.VMEM((GROUP, ROWS, DIM), BF), pltpu.VMEM((GROUP * ROWS, DIM), F32),
            pltpu.VMEM((GROUP * ROWS, DIM), F32), pltpu.VMEM((GROUP, ROWS, DIM), BF), pltpu.VMEM((GROUP, ROWS, DIM), BF),
            pltpu.VMEM((GROUP, GROUP * ROWS, 128), BF), pltpu.VMEM((GROUP, GROUP * ROWS, 128), BF),
            pltpu.VMEM((4, 4, 2, 8, DIM), BF),
            dma((n_loads,)), dma((2, GROUP)), dma((2, GROUP)), dma((2, GROUP)), dma((2, GROUP)),
            dma((64,)), dma((64,)), dma((8,)), dma((8,)), dma((16,)),
        ],
        compiler_params=pltpu.CompilerParams(vmem_limit_bytes=62 * 1024 * 1024, collective_id=0, has_side_effects=True),
        name="two_layers",
    )(lengths, x, freq, ag, kvg, qg, fg, cache0, cache1, wdkv, wqa, wqb, wuk, wuv, wo, wg, wu, wd)


def solution(mesh):
    row_spec = P(("replica", "dp"), None)
    len_spec = P(("replica", "dp"))
    cache_spec = P(("replica", "dp"), None, None)
    in_specs = (row_spec, len_spec, cache_spec, cache_spec) + (P(),) * 13
    out_specs = (P("replica", None), cache_spec, cache_spec)

    def device_step(x_rows, lengths, cache0, cache1, attn_gain, w_dkv, kv_gain, wq_a, q_gain, wq_b, w_uk, w_uv, w_o, ffn_gain, w_gate, w_up, w_down):
        half = ROPE // 2
        inv_freq = 10000.0 ** (-(np.arange(128) % half) / half)
        freq = jnp.asarray(inv_freq[None, :], F32)
        x, ne = two_layers(lengths, x_rows, freq, attn_gain, kv_gain, q_gain, ffn_gain, cache0.transpose(0, 2, 1), cache1.transpose(0, 2, 1),
                           w_dkv.transpose(0, 2, 1), wq_a, wq_b, w_uk, w_uv, w_o, w_gate, w_up, w_down)
        at_slot = lax.broadcasted_iota(jnp.int32, (1, SEQ), 1) == lengths[:, None]
        caches = [jnp.where(at_slot[:, :, None], ne[layer][:, None, :], cache) for layer, cache in enumerate((cache0, cache1))]
        return x.reshape(-1, DIM), caches[0], caches[1]

    return jax.shard_map(device_step, mesh=mesh, in_specs=in_specs, out_specs=out_specs, check_vma=False)
```

time: 345 us -> 73.8 us (0.21)
  waiting for transfers between devices: 195 us -> 0 us
  Pallas kernels: 0 us -> 66.5 us
  matrix products: 62.9 us -> 0 us
  local copies, waits for them, and re-layouts: 29.3 us -> 1.66 us
  blocking collectives: 24.4 us -> 0 us
  between operations: 13.9 us -> 0.64 us
  other arithmetic: 11.6 us -> 4.86 us
  starting transfers between devices: 6.14 us -> 0 us
    all_gather x3 -> x0, waiting for transfers between devices: 181 us -> none  [the longest x2 127 us: device_step(): all_normed = lax.all_gather(normed, 'dp', axis=0, tiled=True)]
    pallas_call x0 -> x1, Pallas kernels: none -> 66.5 us  [two_layers(): pl.pallas_call(step_kernel, out_shape=(jax.ShapeDtypeStruct((4, 4, 2, 8,...]
    dot_general x20 -> x0, matrix products: 62.9 us -> none  [the longest x2 17.2 us: mla_attention(): attn_out = jnp.dot(heads_out, w_o, preferred_element_type=jnp.float32)]
    all_to_all x1 -> x0, blocking collectives: 24.4 us -> none  [device_step(): received = lax.all_to_all(part_sums, 'dp', 0, 0, tiled=True)]
    unnamed x19 -> x3, local copies, waits for them, and re-layouts: 21.9 us -> 0.97 us
    all_to_all x1 -> x0, waiting for transfers between devices: 14.1 us -> none  [device_step(): received = lax.all_to_all(part_sums, 'dp', 0, 0, tiled=True)]
    all_to_all x1 -> x0, starting transfers between devices: 5.83 us -> none  [device_step(): received = lax.all_to_all(part_sums, 'dp', 0, 0, tiled=True)]
    all_to_all x2 -> x0, local copies, waits for them, and re-layouts: 5.05 us -> none  [device_step(): received = lax.all_to_all(part_sums, 'dp', 0, 0, tiled=True)]
  transfers between devices with their start and end apart: 4 -> 0, of which waited for: 4 -> 0; matrix products, arithmetic and copies ran while one was open for 3% -> 0% of each run, Pallas kernels for 0% -> 0%
where the time goes in v2:
time: 73.8 us; the launch traced here: 73.6 us
  Pallas kernels  66.5 us (90%)
  other arithmetic  4.86 us (7%)
  local copies, waits for them, and re-layouts  1.66 us (2%)
    pallas_call x1, Pallas kernels, two_layers(): pl.pallas_call(step_kernel, out_shape=(jax.ShapeDtypeStruct((4, 4, 2, 8,...  66.5 us
    select_n x1, other arithmetic, device_step(): jnp.where(at_slot[:, :, None], ne[layer][:, None, :], cache)  4.13 us

profile of v2, /device:TPU:1, one launch (start us, length us, event | category | flops | bytes accessed | tf_op | source)
XLA Modules:
  0.0 73.6 jit_solution(15031834343916123297)
XLA Ops:
  0.6 0.7 iota_compare_fusion
  1.4 66.5 %two_layers.1 = (bf16[4,4,2,8,2048]{4,3,2,1,0:T(8,128)(2,1)}, bf16[2,2,576]{2,1,0:T(2,128)(2,1)}) custom-call(s32[2]{0:T(128)} %len_ref.1, bf16[2,2048]{1,0:T(2,128)(2,1)} %x_ref.1, f32[1,128]{1,0:T(1,128)} %constant.2.clone.freq_ref, f32[2,2048]{1,0:T(2,128)} %ag_ref.1, f32[2,512]{1,0:T(2,128)} %kvg_ref.1, f32[2,768]{1,0:T(2,128)} %qg_ref.1, ...), custom_call_target="tpu_custom_call" | custom-call | tf_op jit(solution)/shard_map/two_layers/pallas_call | solution.py:355
  67.8 0.7 slice_bitcast_fusion
  68.5 0.0 copy-start
  68.5 4.1 %broadcast_select_fusion = (bf16[2,1024,576]{1,2,0:T(8,128)(2,1)}, bf16[2,1024,576]{1,2,0:T(8,128)(2,1)}) fusion(bf16[2,1024,576]{1,2,0:T(8,128)(2,1)} %param.21, pred[2,1024]{1,0:T(4,128)(4,1)S(1)} %iota_compare_fusion, bf16[2,576]{1,0:T(2,128)(2,1)S(1)} %get-tuple-element.7, bf16[2,1024,576]{1,2,0:T(8,128)(2,1)} %param.20, bf16[2,576]{1,0:T(2,128)(2,1)S(1)} %get-tuple-element.8), kind=kLoop, calls=%fused_computation | loop fusion | flops 2359296 | bytes 9443840 | tf_op jit(solution)/shard_map/jit(_where)/select_n | solution.py:394
  72.6 0.0 copy-done
  72.6 1.0 %copy.22 = bf16[256,2048]{1,0:T(8,128)(2,1)} copy(bf16[256,2048]{1,0:T(8,128)(2,1)S(1)} %bitcast.11) | data formatting | bytes 2097152
Async XLA Ops:
  68.5 4.1 %copy-start = (bf16[4,4,2,8,2048]{4,3,2,1,0:T(8,128)(2,1)S(1)}, bf16[4,4,2,8,2048]{4,3,2,1,0:T(8,128)(2,1)}, u32[]{:S(2)}) copy-start(bf16[4,4,2,8,2048]{4,3,2,1,0:T(8,128)(2,1)} %get-tuple-element.5) | copy-start | bytes 3145732

commit v3 on v2

--- a/solution.py
+++ b/solution.py
@@ -28,11 +28,18 @@
 PAD = 16
 HP = 32
 GROUP = 16
+HALF = DIM // 2
 FS = FFN // GROUP
 QB = 4
-KC = 512
+KC = 1024
 WOC = HEADS * VD // KC
-AHEAD = 13
+AHEAD = 12
+
+
+AT_X, AT_AG, AT_FG, AT_KV = 0, DIM, 2 * DIM, 3 * DIM
+AT_QG = AT_KV + KVR
+AT_FREQ = AT_QG + QR
+AT_LEN = AT_FREQ + 128
 
 
 def rms(v, gain):
@@ -53,10 +60,10 @@
     return pltpu.make_async_remote_copy(src_ref=src, dst_ref=dst, send_sem=send_sem, recv_sem=recv_sem, device_id=dev(peer), device_id_type=MESH)
 
 
-def step_kernel(len_ref, x_ref, freq_ref, ag_ref, kvg_ref, qg_ref, fg_ref, cache0_ref, cache1_ref, wdkv_ref, wqa_ref, wqb_ref, wuk_ref, wuv_ref, wo_ref, wg_ref, wu_ref, wd_ref,
-                out_ref, ne_ref,
-                wdkv, wqa, wqb, wuk, wuv, wo, cbuf, wg, wu, wd, xs, ks, qf, qlat, qrs, of, ob, acc, xm, xg, xf, pf, ps, pr, ps2, pr2, fb,
-                sems, s1, r1, s2, r2, fs, fr, ds, dr, os_):
+def step_kernel(pk_ref, cache0_ref, cache1_ref, wdkv_ref, wqa_ref, wqb_ref, wuk_ref, wuv_ref, wo_ref, wg_ref, wu_ref, wd_ref,
+                out_ref, keep0, keep1,
+                wdkv, wqa, wqb, wuk, wuv, wo, wg, wu, wd, xs, ks, qf, qlat, qrs, of, ob, acc, entry, osend, orecv, xpart, xsend, xm, xg, xf, pf, ps, pr, ps2, pr2, fb,
+                sems, s1, r1, s2, r2, p1, q1, fs, fr, ds, dr, os_):
     idx = lax.axis_index("dp")
     core = lax.rem(idx, 2)
     cx = lax.rem(lax.div(idx, 2), 4)
@@ -80,27 +87,20 @@
     def away(k):
         return index(lax.rem(cz + lax.div(k, 16), 4), lax.rem(cy + lax.rem(lax.div(k, 4), 4), 4), lax.rem(cx + lax.rem(k, 4), 4), core)
 
-    barrier = pltpu.get_barrier_semaphore()
-
-    def greet(k, carry):
-        pl.semaphore_signal(barrier, inc=1, device_id=dev(away(k)), device_id_type=MESH)
-        return carry
-
-    lax.fori_loop(1, 64, greet, 0)
-    for m in range(1, GROUP, 2):
-        pl.semaphore_signal(barrier, inc=1, device_id=dev(flip(m)[1]), device_id_type=MESH)
-
     half = HEADS // 2
     qc = HEADS * QKD // QB
     mine = pl.ds(pl.multiple_of(me * FS, FS), FS)
+    my_half = pl.ds(pl.multiple_of(core * HALF, HALF), HALF)
+    its_half = pl.ds(pl.multiple_of((1 - core) * HALF, HALF), HALF)
+    partner = index(cz, cy, cx, 1 - core)
 
     def loads_of(layer):
         chunks = [(wdkv_ref.at[layer], wdkv), (wqa_ref.at[layer], wqa)]
         chunks += [(wqb_ref.at[layer, :, pl.ds(i * qc, qc)], wqb.at[:, pl.ds(i * qc, qc)]) for i in range(QB)]
         chunks += [(wuk_ref.at[layer, pl.ds(i * half, half)], wuk.at[pl.ds(i * half, half)]) for i in range(2)]
-        chunks += [((cache0_ref, cache1_ref)[layer], cbuf)]
+        chunks += [((cache0_ref, cache1_ref)[layer], (keep0, keep1)[layer])]
         chunks += [(wuv_ref.at[layer, pl.ds(i * half, half)], wuv.at[pl.ds(i * half, half)]) for i in range(2)]
-        chunks += [(wo_ref.at[layer, pl.ds(i * KC, KC)], wo.at[pl.ds(i * KC, KC)]) for i in range(WOC)]
+        chunks += [(wo_ref.at[layer, pl.ds(i * KC, KC), my_half], wo.at[pl.ds(i * KC, KC)]) for i in range(WOC)]
         chunks += [(wg_ref.at[layer, :, mine], wg), (wu_ref.at[layer, :, mine], wu), (wd_ref.at[layer, mine, :], wd)]
         return [pltpu.make_async_copy(s, d, sems.at[i]) for i, (s, d) in enumerate(chunks)]
 
@@ -111,15 +111,28 @@
     for cp in loads[0][:AHEAD]:
         cp.start()
 
+    barrier = pltpu.get_barrier_semaphore()
+
+    def greet(k, carry):
+        pl.semaphore_signal(barrier, inc=1, device_id=dev(away(k)), device_id_type=MESH)
+        return carry
+
+    lax.fori_loop(1, 64, greet, 0)
+    for m in range(1, GROUP, 2):
+        pl.semaphore_signal(barrier, inc=1, device_id=dev(flip(m)[1]), device_id_type=MESH)
+
+
     lane16 = lax.broadcasted_iota(jnp.int32, (PAD, 128), 1)
     row16 = lax.broadcasted_iota(jnp.int32, (PAD, 128), 0)
-    angle = jnp.where(row16 == 0, len_ref[0], len_ref[1]).astype(F32) * freq_ref[...]
+    at_len = [pk_ref[b:b + 1, AT_LEN:AT_LEN + SEQ].astype(jnp.int32) for b in range(ROWS)]
+    angle = jnp.where(row16 == 0, pk_ref[0:1, AT_LEN:AT_LEN + 128], pk_ref[1:2, AT_LEN:AT_LEN + 128]) * pk_ref[0:1, AT_FREQ:AT_FREQ + 128]
     cos_t = jnp.where(lane16 < ROPE, jnp.cos(angle), 0.0)
     sin_t = jnp.sin(angle)
     sin_t = jnp.where(lane16 < ROPE, jnp.where(lane16 < ROPE // 2, -sin_t, sin_t), 0.0)
 
     xs[...] = jnp.zeros_like(xs)
-    xs[0:ROWS, :] = x_ref[...].astype(F32)
+    xs[0:ROWS, :] = pk_ref[:, AT_X:AT_X + DIM]
+    xsend[0] = pk_ref[:, AT_X:AT_X + DIM].astype(BF)
     ks[...] = jnp.zeros_like(ks)
     of[...] = jnp.zeros_like(of)
     for b in range(ROWS):
@@ -127,21 +140,23 @@
         qrs[b, 16:HP, :] = jnp.zeros((HP - 16, 128), F32)
 
     def attention(layer):
+        cbuf = (keep0, keep1)[layer]
+
         def ready(i):
             loads[layer][i].wait()
             if layer == 0 and i + AHEAD < len(loads[0]):
                 loads[0][i + AHEAD].start()
 
-        h = rms(xs[...], ag_ref[layer:layer + 1, :]).astype(BF)
+        h = rms(xs[...], pk_ref[layer:layer + 1, AT_AG:AT_AG + DIM]).astype(BF)
         ready(0)
         k = lax.dot_general(h, wdkv[...], NT, preferred_element_type=F32)
         ready(1)
         qa = jnp.dot(h, wqa[...], preferred_element_type=F32)
-        qa = rms(qa, qg_ref[layer:layer + 1, :]).astype(BF)
+        qa = rms(qa, pk_ref[layer:layer + 1, AT_QG:AT_QG + QR]).astype(BF)
         ks[:, 0:CACHE] = k
-        ks[:, 0:KVR] = rms(k[:, 0:KVR], kvg_ref[layer:layer + 1, :]).astype(BF).astype(F32)
+        ks[:, 0:KVR] = rms(k[:, 0:KVR], pk_ref[layer:layer + 1, AT_KV:AT_KV + KVR]).astype(BF).astype(F32)
         ks[:, KVR:KVR + 128] = rope_lanes(ks[:, KVR:KVR + 128], cos_t, sin_t).astype(BF).astype(F32)
-        ne_ref[layer] = ks[0:ROWS, 0:CACHE].astype(BF)
+        entry[layer] = ks[:, 0:CACHE].astype(BF)
 
         heads_q = HEADS // QB
         qparts = []
@@ -164,7 +179,7 @@
         ol = []
         slot = lax.broadcasted_iota(jnp.int32, (HP, SEQ), 1)
         for b in range(ROWS):
-            p = len_ref[b]
+            p = at_len[b]
             ql = qlat[b].astype(BF)
             qr = rope_lanes(pltpu.roll(qrs[b], 64, 1), cos_t[b:b + 1, :], sin_t[b:b + 1, :]).astype(BF)
             s = jnp.dot(ql, cbuf[b, 0:KVR, :], preferred_element_type=F32)
@@ -187,18 +202,45 @@
             r = jnp.dot(olc, wuv[j], preferred_element_type=F32)
             for b in range(ROWS):
                 of[b:b + 1, j * VD:(j + 1) * VD] = r[b * HP + j:b * HP + j + 1, :]
+        osend[layer] = of[0:ROWS, :].astype(BF)
+        acc[...] = jnp.zeros_like(acc)
+        if layer == 0:
+            pl.semaphore_wait(barrier, 63 + GROUP // 2)
+            cp = remote(xsend.at[0], xpart.at[0], p1.at[0, 1], q1.at[0, 1], partner)
+            cp.start()
+            sent.append(cp)
+        cp = remote(osend.at[layer], orecv.at[layer], p1.at[layer, 0], q1.at[layer, 0], partner)
+        cp.start()
+        sent.append(cp)
+        cp.wait_recv()
+        of[ROWS:2 * ROWS, :] = orecv[layer].astype(F32)
         for i in range(WOC):
             ob[i] = of[:, i * KC:(i + 1) * KC].astype(BF)
-        acc[...] = jnp.zeros_like(acc)
 
         def step(i, carry):
             at = pl.ds(pl.multiple_of(i * KC, KC), KC)
-            pltpu.make_async_copy(wo_ref.at[layer, at], wo.at[at], sems.at[first_wo + i]).wait()
+            pltpu.make_async_copy(wo_ref.at[layer, at, my_half], wo.at[at], sems.at[first_wo + i]).wait()
             acc[...] += jnp.dot(ob[i], wo[at, :], preferred_element_type=F32)
             return carry
 
         lax.fori_loop(0, WOC, step, 0)
-        xm[layer] = (xs[0:ROWS, :] + acc[0:ROWS, :]).astype(BF)
+        remote(xpart.at[layer], xpart.at[layer], p1.at[layer, 1], q1.at[layer, 1], partner).wait_recv()
+        xm[layer, 0:ROWS, :] = (xs[0:ROWS, my_half] + acc[0:ROWS, :]).astype(BF)
+        xm[layer, ROWS:2 * ROWS, :] = (xpart[layer, :, my_half].astype(F32) + acc[ROWS:2 * ROWS, :]).astype(BF)
+
+    def insert(layer):
+        keep = (keep0, keep1)[layer]
+
+        def tile(t, carry):
+            at = pl.ds(pl.multiple_of(t * 128, 128), 128)
+            lane = lax.broadcasted_iota(jnp.int32, (CACHE, 128), 1) + t * 128
+            for b in range(ROWS):
+                hot = jnp.where((row16 == b) & (lane16 + t * 128 == at_len[b][:, 0:128]), 1.0, 0.0).astype(BF)
+                col = lax.dot_general(entry[layer], hot, (((0,), (0,)), ((), ())), preferred_element_type=F32)
+                keep[b, :, at] = jnp.where(lane == at_len[b][:, 0:128], col, keep[b, :, at].astype(F32)).astype(BF)
+            return carry
+
+        lax.fori_loop(0, SEQ // 128, tile, 0)
 
     def group_rows(layer):
         copies = []
@@ -214,8 +256,11 @@
             r, peer = flip(m)
             remote(xm.at[layer], xg.at[r], s1.at[layer, m], r1.at[layer, m], peer).wait_recv()
         for d in range(GROUP):
-            xf[ROWS * d:ROWS * (d + 1), :] = xg[d].astype(F32)
-        g = rms(xf[...], fg_ref[layer:layer + 1, :]).astype(BF)
+            at = pl.ds(d % 2 * HALF, HALF)
+            xf[ROWS * d:ROWS * (d + 1), at] = xg[d, 0:ROWS, :].astype(F32)
+            d2 = d + 1 - 2 * (d % 2)
+            xf[ROWS * d2:ROWS * (d2 + 1), at] = xg[d, ROWS:2 * ROWS, :].astype(F32)
+        g = rms(xf[...], pk_ref[layer:layer + 1, AT_FG:AT_FG + DIM]).astype(BF)
         loads[layer][first_mlp].wait()
         gate = jnp.dot(g, wg[...], preferred_element_type=F32)
         loads[layer][first_mlp + 1].wait()
@@ -224,9 +269,9 @@
         loads[layer][first_mlp + 2].wait()
         pf[...] = jnp.dot(u, wd[...], preferred_element_type=F32)
 
+    sent = []
     attention(0)
-    pl.semaphore_wait(barrier, 63 + GROUP // 2)
-    sent = group_rows(0)
+    sent += group_rows(0)
     for cp in loads[1][:4 + QB]:
         cp.start()
     mlp_share(0)
@@ -240,13 +285,21 @@
     for cp in loads[1][4 + QB:]:
         cp.start()
     pr[me] = ps[me]
+    insert(0)
     for m in range(1, GROUP):
         r, peer = flip(m)
         remote(ps.at[r], pr.at[r], s2.at[0, m], r2.at[0, m], peer).wait_recv()
     total = pr[0].astype(F32)
     for d in range(1, GROUP):
         total += pr[d].astype(F32)
-    xs[0:ROWS, :] = (xm[0].astype(F32) + total).astype(BF).astype(F32)
+    xs[0:ROWS, my_half] = xg[me, 0:ROWS, :].astype(F32)
+    xs[0:ROWS, its_half] = xg[me + 1 - 2 * core, ROWS:2 * ROWS, :].astype(F32)
+    new_x = (xs[0:ROWS, :] + total).astype(BF)
+    xsend[1] = new_x
+    xs[0:ROWS, :] = new_x.astype(F32)
+    cp = remote(xsend.at[1], xpart.at[1], p1.at[1, 1], q1.at[1, 1], partner)
+    cp.start()
+    sent.append(cp)
 
     attention(1)
     sent += group_rows(1)
@@ -294,7 +347,7 @@
         return carry
 
     lax.fori_loop(0, 64, spread, 0)
-    partner = index(cz, cy, cx, 1 - core)
+    insert(1)
 
     def gathered(t, carry):
         z = lax.rem(gz + lax.div(t, 4), 2)
@@ -347,34 +400,34 @@
     lax.fori_loop(0, 8, finish, 0)
 
 
-def two_layers(lengths, x, freq, ag, kvg, qg, fg, cache0, cache1, wdkv, wqa, wqb, wuk, wuv, wo, wg, wu, wd):
+def two_layers(pk, cache0, cache1, wdkv, wqa, wqb, wuk, wuv, wo, wg, wu, wd):
     vm = pl.BlockSpec(memory_space=pltpu.VMEM)
     anyspec = pl.BlockSpec(memory_space=pl.ANY)
     dma = pltpu.SemaphoreType.DMA
     n_loads = 5 + QB + 2 + WOC + 3
     return pl.pallas_call(
         step_kernel,
-        out_shape=(jax.ShapeDtypeStruct((4, 4, 2, 8, DIM), BF), jax.ShapeDtypeStruct((2, ROWS, CACHE), BF)),
-        in_specs=[pl.BlockSpec(memory_space=pltpu.SMEM)] + [vm] * 6 + [anyspec] * 11,
-        out_specs=(anyspec, vm),
+        out_shape=(jax.ShapeDtypeStruct((4, 4, 2, 8, DIM), BF),) + (jax.ShapeDtypeStruct((ROWS, CACHE, SEQ), BF),) * 2,
+        in_specs=[vm] + [pl.BlockSpec(memory_space=pltpu.HBM)] * 11,
+        out_specs=(anyspec, vm, vm),
         scratch_shapes=[
             pltpu.VMEM((CACHE, DIM), BF), pltpu.VMEM((DIM, QR), BF), pltpu.VMEM((QR, HEADS * QKD), BF),
-            pltpu.VMEM((HEADS, NOPE, KVR), BF), pltpu.VMEM((HEADS, KVR, VD), BF), pltpu.VMEM((HEADS * VD, DIM), BF),
-            pltpu.VMEM((ROWS, CACHE, SEQ), BF),
+            pltpu.VMEM((HEADS, NOPE, KVR), BF), pltpu.VMEM((HEADS, KVR, VD), BF), pltpu.VMEM((HEADS * VD, HALF), BF),
             pltpu.VMEM((DIM, FS), BF), pltpu.VMEM((DIM, FS), BF), pltpu.VMEM((FS, DIM), BF),
             pltpu.VMEM((PAD, DIM), F32), pltpu.VMEM((PAD, KVR + 128), F32),
             pltpu.VMEM((PAD, HEADS * QKD), F32), pltpu.VMEM((ROWS, HP, KVR), F32), pltpu.VMEM((ROWS, HP, 128), F32),
-            pltpu.VMEM((PAD, HEADS * VD), F32), pltpu.VMEM((WOC, PAD, KC), BF), pltpu.VMEM((PAD, DIM), F32),
-            pltpu.VMEM((2, ROWS, DIM), BF), pltpu.VMEM((GROUP, ROWS, DIM), BF), pltpu.VMEM((GROUP * ROWS, DIM), F32),
+            pltpu.VMEM((PAD, HEADS * VD), F32), pltpu.VMEM((WOC, PAD, KC), BF), pltpu.VMEM((PAD, HALF), F32), pltpu.VMEM((2, PAD, CACHE), BF),
+            pltpu.VMEM((2, ROWS, HEADS * VD), BF), pltpu.VMEM((2, ROWS, HEADS * VD), BF), pltpu.VMEM((2, ROWS, DIM), BF), pltpu.VMEM((2, ROWS, DIM), BF),
+            pltpu.VMEM((2, 2 * ROWS, HALF), BF), pltpu.VMEM((GROUP, 2 * ROWS, HALF), BF), pltpu.VMEM((GROUP * ROWS, DIM), F32),
             pltpu.VMEM((GROUP * ROWS, DIM), F32), pltpu.VMEM((GROUP, ROWS, DIM), BF), pltpu.VMEM((GROUP, ROWS, DIM), BF),
             pltpu.VMEM((GROUP, GROUP * ROWS, 128), BF), pltpu.VMEM((GROUP, GROUP * ROWS, 128), BF),
             pltpu.VMEM((4, 4, 2, 8, DIM), BF),
             dma((n_loads,)), dma((2, GROUP)), dma((2, GROUP)), dma((2, GROUP)), dma((2, GROUP)),
-            dma((64,)), dma((64,)), dma((8,)), dma((8,)), dma((16,)),
+            dma((2, 2)), dma((2, 2)), dma((64,)), dma((64,)), dma((8,)), dma((8,)), dma((16,)),
         ],
-        compiler_params=pltpu.CompilerParams(vmem_limit_bytes=62 * 1024 * 1024, collective_id=0, has_side_effects=True),
+        compiler_params=pltpu.CompilerParams(vmem_limit_bytes=48 * 1024 * 1024, collective_id=0, has_side_effects=True),
         name="two_layers",
-    )(lengths, x, freq, ag, kvg, qg, fg, cache0, cache1, wdkv, wqa, wqb, wuk, wuv, wo, wg, wu, wd)
+    )(pk, cache0, cache1, wdkv, wqa, wqb, wuk, wuv, wo, wg, wu, wd)
 
 
 def solution(mesh):
@@ -387,11 +440,16 @@
     def device_step(x_rows, lengths, cache0, cache1, attn_gain, w_dkv, kv_gain, wq_a, q_gain, wq_b, w_uk, w_uv, w_o, ffn_gain, w_gate, w_up, w_down):
         half = ROPE // 2
         inv_freq = 10000.0 ** (-(np.arange(128) % half) / half)
-        freq = jnp.asarray(inv_freq[None, :], F32)
-        x, ne = two_layers(lengths, x_rows, freq, attn_gain, kv_gain, q_gain, ffn_gain, cache0.transpose(0, 2, 1), cache1.transpose(0, 2, 1),
+        freq = jnp.broadcast_to(jnp.asarray(inv_freq[None, :], F32), (2, 128))
+        lens = jnp.broadcast_to(lengths.astype(F32)[:, None], (ROWS, SEQ))
+        pk, at = 0.0, 0
+        pieces = [x_rows.astype(F32), attn_gain, ffn_gain, kv_gain, q_gain, freq, lens]
+        width = sum(piece.shape[1] for piece in pieces)
+        for piece in pieces:
+            pk = pk + jnp.pad(piece, ((0, 0), (at, width - at - piece.shape[1])))
+            at += piece.shape[1]
+        x, *kept = two_layers(pk, cache0.transpose(0, 2, 1), cache1.transpose(0, 2, 1),
                            w_dkv.transpose(0, 2, 1), wq_a, wq_b, w_uk, w_uv, w_o, w_gate, w_up, w_down)
-        at_slot = lax.broadcasted_iota(jnp.int32, (1, SEQ), 1) == lengths[:, None]
-        caches = [jnp.where(at_slot[:, :, None], ne[layer][:, None, :], cache) for layer, cache in enumerate((cache0, cache1))]
-        return x.reshape(-1, DIM), caches[0], caches[1]
+        return x.reshape(-1, DIM), kept[0].transpose(0, 2, 1), kept[1].transpose(0, 2, 1)
 
     return jax.shard_map(device_step, mesh=mesh, in_specs=in_specs, out_specs=out_specs, check_vma=False)

time: 73.8 us -> 67.7 us (0.917)
  Pallas kernels: 66.5 us -> 61.5 us
  other arithmetic: 4.86 us -> 1.53 us
  local copies, waits for them, and re-layouts: 1.66 us -> 3.86 us
    pallas_call x1, Pallas kernels: 66.5 us -> 61.5 us  [two_layers(): pl.pallas_call(step_kernel, out_shape=(jax.ShapeDtypeStruct((4, 4, 2, 8,...]
    select_n x1 -> x0, other arithmetic: 4.13 us -> none  [device_step(): jnp.where(at_slot[:, :, None], ne[layer][:, None, :], cache)]
    unnamed x3, local copies, waits for them, and re-layouts: 0.97 us -> 3.78 us
    add x0 -> x1, other arithmetic: none -> 0.88 us  [device_step(): pk = pk + jnp.pad(piece, ((0, 0), (at, width - at - piece.shape[1])))]
where the time goes in v3:
time: 67.7 us; the launch traced here: 67.5 us
  Pallas kernels  61.5 us (91%)
  local copies, waits for them, and re-layouts  3.86 us (6%)
  other arithmetic  1.53 us (2%)
    pallas_call x1, Pallas kernels, two_layers(): pl.pallas_call(step_kernel, out_shape=(jax.ShapeDtypeStruct((4, 4, 2, 8,...  61.5 us
    unnamed x3, local copies, waits for them, and re-layouts  3.78 us

profile of v3, /device:TPU:1, one launch (start us, length us, event | category | flops | bytes accessed | tf_op | source)
XLA Modules:
  0.0 67.5 jit_solution(7580122462206364110)
XLA Ops:
  0.6 0.7 convert_element_type.18
  1.3 0.1 broadcast_in_dim.5
  1.4 0.9 %pad_add_fusion.pk_ref = f32[2,8576]{1,0:T(2,128)S(1)} fusion(f32[2,1024]{1,0:T(2,128)S(1)} %broadcast_in_dim.5, f32[2,768]{1,0:T(2,128)} %param.26, f32[2,512]{1,0:T(2,128)} %param.24, f32[2,2048]{1,0:T(2,128)} %param.31, f32[2,2048]{1,0:T(2,128)} %param.22, f32[8576]{0:T(1024)} %constant.27, bf16[2,2048]{1,0:T(2,128)(2,1)} %param.18), kind=kLoop, calls=%fused_computation | loop fusion | flops 120064 | bytes 162304 | tf_op jit(solution)/shard_map/add | solution.py:449
  2.2 61.5 %two_layers.1 = (bf16[4,4,2,8,2048]{4,3,2,1,0:T(8,128)(2,1)S(1)}, bf16[2,576,1024]{2,1,0:T(8,128)(2,1)S(1)}, bf16[2,576,1024]{2,1,0:T(8,128)(2,1)S(1)}) custom-call(f32[2,8576]{1,0:T(2,128)S(1)} %pad_add_fusion.pk_ref, bf16[2,576,1024]{2,1,0:T(8,128)(2,1)} %bitcast.10, bf16[2,576,1024]{2,1,0:T(8,128)(2,1)} %bitcast.11, bf16[2,576,2048]{2,1,0:T(8,128)(2,1)} %bitcast.9, ...), custom_call_target="tpu_custom_call" | custom-call | tf_op jit(solution)/shard_map/two_layers/pallas_call | solution.py:408
  63.7 1.0 %copy.24 = bf16[256,2048]{1,0:T(8,128)(2,1)} copy(bf16[256,2048]{1,0:T(8,128)(2,1)S(1)} %bitcast.8) | data formatting | bytes 2097152
  64.7 1.4 %copy.25 = bf16[2,1024,576]{1,2,0:T(8,128)(2,1)} copy(bf16[2,1024,576]{1,2,0:T(8,128)(2,1)S(1)} %bitcast.7) | data formatting | bytes 4718592
  66.1 1.4 %copy.26 = bf16[2,1024,576]{1,2,0:T(8,128)(2,1)} copy(bf16[2,1024,576]{1,2,0:T(8,128)(2,1)S(1)} %bitcast.6) | data formatting | bytes 4718592

commit v4 on v3

--- a/solution.py
+++ b/solution.py
@@ -62,8 +62,8 @@
 
 def step_kernel(pk_ref, cache0_ref, cache1_ref, wdkv_ref, wqa_ref, wqb_ref, wuk_ref, wuv_ref, wo_ref, wg_ref, wu_ref, wd_ref,
                 out_ref, keep0, keep1,
-                wdkv, wqa, wqb, wuk, wuv, wo, wg, wu, wd, xs, ks, qf, qlat, qrs, of, ob, acc, entry, osend, orecv, xpart, xsend, xm, xg, xf, pf, ps, pr, ps2, pr2, fb,
-                sems, s1, r1, s2, r2, p1, q1, fs, fr, ds, dr, os_):
+                wdkv, wqa, wqb, wuk, wuv, wo, wg, wu, wd, xs, ks, qf, qlat, qrs, of, ob, acc, entry, osend, orecv, xpart, xsend, xm, xg, xf, pf, ps, pr, ps2, pr2,
+                sems, s1, r1, s2, r2, p1, q1, fs, fr, ds, dr):
     idx = lax.axis_index("dp")
     core = lax.rem(idx, 2)
     cx = lax.rem(lax.div(idx, 2), 4)
@@ -324,7 +324,7 @@
     fin = (xf[:, cols(chip, core)] + total).astype(BF)
     for z in range(2):
         for y in range(2):
-            fb[gz * 2 + z, gy * 2 + y, gx, :, cols(chip, core)] = fin[(z * 2 + y) * 8:(z * 2 + y) * 8 + 8, :]
+            out_ref[gz * 2 + z, gy * 2 + y, gx, :, cols(chip, core)] = fin[(z * 2 + y) * 8:(z * 2 + y) * 8 + 8, :]
 
     def block(ref, z, y, x, c):
         q = lax.rem(z, 2) * 4 + lax.rem(y, 2) * 2 + lax.rem(x, 2)
@@ -333,7 +333,7 @@
     def side(ref, z, y, x, c):
         return ref.at[pl.ds(z * 2, 2), pl.ds(y * 2, 2), x, :, pl.ds(pl.multiple_of(c * 1024, 1024), 1024)]
 
-    own_block = block(fb, cz, cy, cx, core)
+    own_block = block(out_ref, cz, cy, cx, core)
 
     def digit(a):
         return lax.rem(2 + 3 * a, 4)
@@ -360,13 +360,12 @@
 
             @pl.when(k != 0)
             def _():
-                remote(own_block, block(fb, oz, oy, ox, core), fs.at[k], fr.at[k], index(oz, oy, ox, core)).wait_recv()
+                remote(own_block, block(out_ref, oz, oy, ox, core), fs.at[k], fr.at[k], index(oz, oy, ox, core)).wait_recv()
             return carry
 
         lax.fori_loop(0, 8, arrive, 0)
-        part = side(fb, z, y, x, core)
+        part = side(out_ref, z, y, x, core)
         remote(part, part, ds.at[t], dr.at[t], partner).start()
-        pltpu.make_async_copy(part, side(out_ref, z, y, x, core), os_.at[t]).start()
         return carry
 
     lax.fori_loop(0, 8, gathered, 0)
@@ -375,9 +374,8 @@
         z = lax.rem(gz + lax.div(t, 4), 2)
         y = lax.rem(gy + lax.rem(lax.div(t, 2), 2), 2)
         x = lax.rem(gx + lax.rem(t, 2), 2)
-        part = side(fb, z, y, x, 1 - core)
+        part = side(out_ref, z, y, x, 1 - core)
         remote(part, part, ds.at[t], dr.at[t], partner).wait_recv()
-        pltpu.make_async_copy(part, side(out_ref, z, y, x, 1 - core), os_.at[8 + t]).start()
         return carry
 
     lax.fori_loop(0, 8, passed, 0)
@@ -391,10 +389,8 @@
     lax.fori_loop(1, 64, sent_block, 0)
 
     def finish(t, carry):
-        part = side(fb, 0, 0, 0, core)
+        part = side(out_ref, 0, 0, 0, core)
         remote(part, part, ds.at[t], dr.at[t], partner).wait_send()
-        pltpu.make_async_copy(part, side(out_ref, 0, 0, 0, core), os_.at[t]).wait()
-        pltpu.make_async_copy(part, side(out_ref, 0, 0, 0, core), os_.at[8 + t]).wait()
         return carry
 
     lax.fori_loop(0, 8, finish, 0)
@@ -402,14 +398,13 @@
 
 def two_layers(pk, cache0, cache1, wdkv, wqa, wqb, wuk, wuv, wo, wg, wu, wd):
     vm = pl.BlockSpec(memory_space=pltpu.VMEM)
-    anyspec = pl.BlockSpec(memory_space=pl.ANY)
     dma = pltpu.SemaphoreType.DMA
     n_loads = 5 + QB + 2 + WOC + 3
     return pl.pallas_call(
         step_kernel,
         out_shape=(jax.ShapeDtypeStruct((4, 4, 2, 8, DIM), BF),) + (jax.ShapeDtypeStruct((ROWS, CACHE, SEQ), BF),) * 2,
         in_specs=[vm] + [pl.BlockSpec(memory_space=pltpu.HBM)] * 11,
-        out_specs=(anyspec, vm, vm),
+        out_specs=(vm, vm, vm),
         scratch_shapes=[
             pltpu.VMEM((CACHE, DIM), BF), pltpu.VMEM((DIM, QR), BF), pltpu.VMEM((QR, HEADS * QKD), BF),
             pltpu.VMEM((HEADS, NOPE, KVR), BF), pltpu.VMEM((HEADS, KVR, VD), BF), pltpu.VMEM((HEADS * VD, HALF), BF),
@@ -421,13 +416,33 @@
             pltpu.VMEM((2, 2 * ROWS, HALF), BF), pltpu.VMEM((GROUP, 2 * ROWS, HALF), BF), pltpu.VMEM((GROUP * ROWS, DIM), F32),
             pltpu.VMEM((GROUP * ROWS, DIM), F32), pltpu.VMEM((GROUP, ROWS, DIM), BF), pltpu.VMEM((GROUP, ROWS, DIM), BF),
             pltpu.VMEM((GROUP, GROUP * ROWS, 128), BF), pltpu.VMEM((GROUP, GROUP * ROWS, 128), BF),
-            pltpu.VMEM((4, 4, 2, 8, DIM), BF),
             dma((n_loads,)), dma((2, GROUP)), dma((2, GROUP)), dma((2, GROUP)), dma((2, GROUP)),
-            dma((2, 2)), dma((2, 2)), dma((64,)), dma((64,)), dma((8,)), dma((8,)), dma((16,)),
+            dma((2, 2)), dma((2, 2)), dma((64,)), dma((64,)), dma((8,)), dma((8,)),
         ],
         compiler_params=pltpu.CompilerParams(vmem_limit_bytes=48 * 1024 * 1024, collective_id=0, has_side_effects=True),
         name="two_layers",
     )(pk, cache0, cache1, wdkv, wqa, wqb, wuk, wuv, wo, wg, wu, wd)
+
+
+def write_kernel(x_ref, c0_ref, c1_ref, xo_ref, o0_ref, o1_ref, sems):
+    pairs = [(x_ref, xo_ref)] + [(c.at[b], o.at[b]) for c, o in ((c0_ref, o0_ref), (c1_ref, o1_ref)) for b in range(ROWS)]
+    copies = [pltpu.make_async_copy(s, d, sems.at[i]) for i, (s, d) in enumerate(pairs)]
+    for cp in copies:
+        cp.start()
+    for cp in copies:
+        cp.wait()
+
+
+def write_out(x, c0, c1):
+    return pl.pallas_call(
+        write_kernel,
+        out_shape=tuple(jax.ShapeDtypeStruct(v.shape, v.dtype) for v in (x, c0, c1)),
+        in_specs=[pl.BlockSpec(memory_space=pltpu.VMEM)] * 3,
+        out_specs=(pl.BlockSpec(memory_space=pltpu.HBM),) * 3,
+        scratch_shapes=[pltpu.SemaphoreType.DMA((1 + 2 * ROWS,))],
+        compiler_params=pltpu.CompilerParams(vmem_limit_bytes=16 * 1024 * 1024),
+        name="write_out",
+    )(x, c0, c1)
 
 
 def solution(mesh):
@@ -450,6 +465,7 @@
             at += piece.shape[1]
         x, *kept = two_layers(pk, cache0.transpose(0, 2, 1), cache1.transpose(0, 2, 1),
                            w_dkv.transpose(0, 2, 1), wq_a, wq_b, w_uk, w_uv, w_o, w_gate, w_up, w_down)
+        x, *kept = write_out(x, *kept)
         return x.reshape(-1, DIM), kept[0].transpose(0, 2, 1), kept[1].transpose(0, 2, 1)
 
     return jax.shard_map(device_step, mesh=mesh, in_specs=in_specs, out_specs=out_specs, check_vma=False)

time: 67.7 us -> 66.1 us (0.976)
  local copies, waits for them, and re-layouts: 3.86 us -> 0.07 us
  Pallas kernels: 61.5 us -> 63.6 us
    unnamed x3 -> x0, local copies, waits for them, and re-layouts: 3.78 us -> none
    pallas_call x0 -> x1, Pallas kernels: none -> 2.57 us  [write_out(): pl.pallas_call(write_kernel, out_shape=tuple((jax.ShapeDtypeStruct(v.shap...]
where the time goes in v4:
time: 66.1 us; the launch traced here: 65.9 us
  Pallas kernels  63.6 us (96%)
  other arithmetic  1.53 us (2%)
    pallas_call x1, Pallas kernels, two_layers(): pl.pallas_call(step_kernel, out_shape=(jax.ShapeDtypeStruct((4, 4, 2, 8,...  61.1 us
    pallas_call x1, Pallas kernels, write_out(): pl.pallas_call(write_kernel, out_shape=tuple((jax.ShapeDtypeStruct(v.shap...  2.57 us

profile of v4, /device:TPU:1, one launch (start us, length us, event | category | flops | bytes accessed | tf_op | source)
XLA Modules:
  0.0 65.9 jit_solution(1690791691102165934)
XLA Ops:
  0.6 0.7 convert_element_type.18
  1.3 0.1 broadcast_in_dim.5
  1.4 0.9 %pad_add_fusion.pk_ref = f32[2,8576]{1,0:T(2,128)S(1)} fusion(f32[2,1024]{1,0:T(2,128)S(1)} %broadcast_in_dim.5, f32[2,768]{1,0:T(2,128)} %param.26, f32[2,512]{1,0:T(2,128)} %param.24, f32[2,2048]{1,0:T(2,128)} %param.31, f32[2,2048]{1,0:T(2,128)} %param.22, f32[8576]{0:T(1024)} %constant.27, bf16[2,2048]{1,0:T(2,128)(2,1)} %param.18), kind=kLoop, calls=%fused_computation | loop fusion | flops 120064 | bytes 162304 | tf_op jit(solution)/shard_map/add | solution.py:464
  2.2 61.1 %two_layers.1 = (bf16[4,4,2,8,2048]{4,3,2,1,0:T(8,128)(2,1)S(1)}, bf16[2,576,1024]{2,1,0:T(8,128)(2,1)S(1)}, bf16[2,576,1024]{2,1,0:T(8,128)(2,1)S(1)}) custom-call(f32[2,8576]{1,0:T(2,128)S(1)} %pad_add_fusion.pk_ref, bf16[2,576,1024]{2,1,0:T(8,128)(2,1)} %bitcast.7, bf16[2,576,1024]{2,1,0:T(8,128)(2,1)} %bitcast.8, bf16[2,576,2048]{2,1,0:T(8,128)(2,1)} %bitcast.6, ...), custom_call_target="tpu_custom_call" | custom-call | tf_op jit(solution)/shard_map/two_layers/pallas_call | solution.py:403
  63.3 2.6 %write_out.1 = (bf16[4,4,2,8,2048]{4,3,2,1,0:T(8,128)(2,1)}, bf16[2,576,1024]{2,1,0:T(8,128)(2,1)}, bf16[2,576,1024]{2,1,0:T(8,128)(2,1)}) custom-call(bf16[4,4,2,8,2048]{4,3,2,1,0:T(8,128)(2,1)S(1)} %get-tuple-element.9.x_ref, bf16[2,576,1024]{2,1,0:T(8,128)(2,1)S(1)} %get-tuple-element.10.c0_ref, bf16[2,576,1024]{2,1,0:T(8,128)(2,1)S(1)} %get-tuple-element.11.c1_ref), custom_call_target="tpu_custom_call" | custom-call | tf_op jit(solution)/shard_map/write_out/pallas_call | solution.py:437
